TPU v7x, 8 devices: a whole 2x2x1 slice. The times are simulated.
8 devices in a mesh: dp: 1 (over z), tp: 8 (over y, x, core).
Axes of the slice: x: 2, y: 2, z: 1, core: 2. Of those that a mesh axis runs over, the one named last changes fastest.
Arguments:
- x_steps: bfloat16 [32, 64, 2048], P(None, 'dp')
- cur_len: int32 [64], P('dp')
- k_cache: bfloat16 [2, 64, 128, 16, 128], P(None, 'dp', None, 'tp')
- v_cache: bfloat16 [2, 64, 128, 16, 128], P(None, 'dp', None, 'tp')
- ln_gain: bfloat16 [2, 2048], replicated
- ln_bias: bfloat16 [2, 2048], replicated
- w_q: bfloat16 [2, 2048, 2048], P(None, None, 'tp')
- w_k: bfloat16 [2, 2048, 2048], P(None, None, 'tp')
- w_v: bfloat16 [2, 2048, 2048], P(None, None, 'tp')
- w_o: bfloat16 [2, 2048, 2048], P(None, 'tp')
- w_in: bfloat16 [2, 2048, 8192], P(None, None, 'tp')
- b_in: bfloat16 [2, 8192], P(None, 'tp')
- w_out: bfloat16 [2, 8192, 2048], P(None, 'tp')
- b_out: bfloat16 [2, 2048], replicated
Outputs:
- output 1: bfloat16 [32, 64, 2048], P(None, 'dp')
- output 2: bfloat16 [2, 64, 128, 16, 128], P(None, 'dp', None, 'tp')
- output 3: bfloat16 [2, 64, 128, 16, 128], P(None, 'dp', None, 'tp')
All inputs are finite; a program needn't handle non-finite values.
Results may differ from a plain program's by a relative error of at most 0.0160624.
Values are sent between devices in bfloat16 or wider.
A program may use at most 1 GiB of HBM per device.

v0:
```python
import jax
import jax.numpy as jnp
from jax import lax
from jax.sharding import PartitionSpec as P

ROT_DIM = 64
LN_EPS = 1e-5


def layer_norm(hidden, gain, bias):
    hid_f32 = hidden.astype(jnp.float32)
    row_mean = jnp.mean(hid_f32, axis=-1, keepdims=True)
    centered = hid_f32 - row_mean
    row_var = jnp.mean(centered * centered, axis=-1, keepdims=True)
    normed = centered * lax.rsqrt(row_var + LN_EPS)
    return (normed * gain.astype(jnp.float32) + bias.astype(jnp.float32)).astype(jnp.bfloat16)


def rotary_tables(positions):
    inv_freq = 1.0 / (10000.0 ** (jnp.arange(0, ROT_DIM, 2).astype(jnp.float32) / ROT_DIM))
    angles = positions.astype(jnp.float32)[:, None] * inv_freq[None, :]
    return jnp.cos(angles)[:, None, :], jnp.sin(angles)[:, None, :]


def apply_rotary(vectors, cos_tab, sin_tab):
    lead_shape = vectors.shape[:-1]
    pairs = vectors[..., :ROT_DIM].reshape(lead_shape + (ROT_DIM // 2, 2))
    even_part = pairs[..., 0]
    odd_part = pairs[..., 1]
    rotated = jnp.stack([even_part * cos_tab - odd_part * sin_tab, odd_part * cos_tab + even_part * sin_tab], axis=-1)
    return jnp.concatenate([rotated.reshape(lead_shape + (ROT_DIM,)), vectors[..., ROT_DIM:]], axis=-1)


def attend(query, k_layer, v_layer, visible):
    score_scale = k_layer.shape[-1] ** -0.5
    scores = jnp.einsum("bhe,bshe->bhs", query, k_layer, preferred_element_type=jnp.float32) * score_scale
    scores = jnp.where(visible, scores, -jnp.inf)
    exp_scores = jnp.exp(scores - jnp.max(scores, axis=-1, keepdims=True))
    attn_probs = (exp_scores / jnp.sum(exp_scores, axis=-1, keepdims=True)).astype(jnp.bfloat16)
    context = jnp.einsum("bhs,bshe->bhe", attn_probs, v_layer, preferred_element_type=jnp.float32)
    return context.astype(jnp.bfloat16)


def step_setup(cur_len, step_idx, cache_len):
    new_pos = cur_len + step_idx
    slot_ids = jnp.arange(cache_len)
    visible = (slot_ids[None, :] <= new_pos[:, None])[:, None, :]
    return new_pos, rotary_tables(new_pos), visible


def layer_update(normed, new_pos, rotary, visible, caches, layer_idx, weights):
    cos_tab, sin_tab = rotary
    k_cache, v_cache = caches
    q_weight, k_weight, v_weight, o_weight, in_weight, in_bias, out_weight = weights
    batch = normed.shape[0]
    n_heads = k_cache.shape[3]
    head_dim = k_cache.shape[4]
    head_shape = (batch, n_heads, head_dim)
    query = jnp.dot(normed, q_weight, preferred_element_type=jnp.float32).reshape(head_shape)
    key_new = jnp.dot(normed, k_weight, preferred_element_type=jnp.float32).reshape(head_shape)
    value_new = jnp.dot(normed, v_weight, preferred_element_type=jnp.float32).astype(jnp.bfloat16).reshape(head_shape)
    query = apply_rotary(query, cos_tab, sin_tab).astype(jnp.bfloat16)
    key_new = apply_rotary(key_new, cos_tab, sin_tab).astype(jnp.bfloat16)
    batch_rows = jnp.arange(batch)
    k_cache = k_cache.at[layer_idx, batch_rows, new_pos].set(key_new)
    v_cache = v_cache.at[layer_idx, batch_rows, new_pos].set(value_new)
    context = attend(query, k_cache[layer_idx], v_cache[layer_idx], visible).reshape(batch, n_heads * head_dim)
    pre_act = jnp.dot(normed, in_weight, preferred_element_type=jnp.float32) + in_bias.astype(jnp.float32)
    gelu_act = jax.nn.gelu(pre_act, approximate=True).astype(jnp.bfloat16)
    layer_part = jnp.dot(context, o_weight, preferred_element_type=jnp.float32) + jnp.dot(gelu_act, out_weight, preferred_element_type=jnp.float32)
    return layer_part, k_cache, v_cache


def decode_shard(x_steps, cur_len, k_cache, v_cache, ln_gain, ln_bias, w_q, w_k, w_v, w_o, w_in, b_in, w_out, b_out):
    n_layers = k_cache.shape[0]
    outputs = []
    for step_idx in range(x_steps.shape[0]):
        new_pos, rotary, visible = step_setup(cur_len, step_idx, k_cache.shape[2])
        hidden = x_steps[step_idx]
        for layer_idx in range(n_layers):
            normed = layer_norm(hidden, ln_gain[layer_idx], ln_bias[layer_idx])
            weights = (w_q[layer_idx], w_k[layer_idx], w_v[layer_idx], w_o[layer_idx], w_in[layer_idx], b_in[layer_idx], w_out[layer_idx])
            layer_part, k_cache, v_cache = layer_update(normed, new_pos, rotary, visible, (k_cache, v_cache), layer_idx, weights)
            layer_sum = lax.psum(layer_part.astype(jnp.bfloat16), "tp")
            hidden = (hidden.astype(jnp.float32) + layer_sum.astype(jnp.float32) + b_out[layer_idx].astype(jnp.float32)).astype(jnp.bfloat16)
        outputs.append(hidden)
    return jnp.stack(outputs), k_cache, v_cache


def solution(mesh):
    cache_spec = P(None, "dp", None, "tp", None)
    in_specs = (P(None, "dp", None), P("dp"), cache_spec, cache_spec, P(None, None), P(None, None),
                P(None, None, "tp"), P(None, None, "tp"), P(None, None, "tp"), P(None, "tp", None),
                P(None, None, "tp"), P(None, "tp"), P(None, "tp", None), P(None, None))
    out_specs = (P(None, "dp", None), cache_spec, cache_spec)
    return jax.shard_map(decode_shard, mesh=mesh, in_specs=in_specs, out_specs=out_specs, check_vma=False)
```

profile of v0, /device:TPU:0, one launch (start us, length us, event | category | flops | bytes accessed | tf_op | source)
XLA Modules:
  0.0 5793.5 jit_solution(1378329683170054316)
XLA Ops:
  879.7 10.4 slice_bitcast_fusion.124
  929.4 10.4 slice_bitcast_fusion.122
  962.5 39.5 all-reduce.37.cloned.1.call-done
  1086.4 10.4 slice_bitcast_fusion.118
  1118.0 36.1 all-reduce.39.cloned.1.call-done
  1237.4 10.6 slice_bitcast_fusion.114
  1268.3 36.2 all-reduce.41.cloned.1.call-done
  1387.8 10.6 slice_bitcast_fusion.110
  1418.8 36.2 all-reduce.43.cloned.1.call-done
  1538.2 10.6 slice_bitcast_fusion.106
  1569.2 36.1 all-reduce.45.cloned.1.call-done
  1687.9 10.6 slice_bitcast_fusion.102
  1718.9 36.2 all-reduce.47.cloned.1.call-done
  1837.6 10.6 slice_bitcast_fusion.98
  1867.9 36.2 all-reduce.49.cloned.1.call-done
  1987.3 10.6 slice_bitcast_fusion.94
  2017.6 36.2 all-reduce.51.cloned.1.call-done
  2137.0 10.6 slice_bitcast_fusion.90
  2167.2 36.2 all-reduce.53.cloned.1.call-done
  2286.6 10.6 slice_bitcast_fusion.86
  2316.9 36.1 all-reduce.55.cloned.1.call-done
  2436.3 10.6 slice_bitcast_fusion.82
  2466.5 36.1 all-reduce.57.cloned.1.call-done
  2585.9 10.6 slice_bitcast_fusion.78
  2616.2 36.2 all-reduce.59.cloned.1.call-done
  2735.6 10.6 slice_bitcast_fusion.74
  2765.8 36.2 all-reduce.61.cloned.1.call-done
  2885.2 10.6 slice_bitcast_fusion.70
  2915.4 36.1 all-reduce.63.cloned.1.call-done
  3034.8 10.6 slice_bitcast_fusion.66
  3065.1 36.1 all-reduce.65.cloned.1.call-done
  3184.5 10.6 slice_bitcast_fusion.62
  3214.7 36.2 all-reduce.67.cloned.1.call-done
  3334.1 10.6 slice_bitcast_fusion.58
  3364.4 36.1 all-reduce.69.cloned.1.call-done
  3483.8 10.6 slice_bitcast_fusion.54
  3514.0 36.2 all-reduce.71.cloned.1.call-done
  3633.4 10.6 slice_bitcast_fusion.50
  3663.7 36.1 all-reduce.73.cloned.1.call-done
  3783.1 10.6 slice_bitcast_fusion.46
  3813.3 36.1 all-reduce.75.cloned.1.call-done
  3932.7 10.6 slice_bitcast_fusion.42
  3963.0 36.2 all-reduce.77.cloned.1.call-done
  4082.4 10.6 slice_bitcast_fusion.38
  4112.7 36.1 all-reduce.79.cloned.1.call-done
  4232.1 10.6 slice_bitcast_fusion.34
  4262.4 36.2 all-reduce.81.cloned.1.call-done
  4381.8 10.6 slice_bitcast_fusion.30
  4412.1 36.1 all-reduce.83.cloned.1.call-done
  4531.5 10.6 slice_bitcast_fusion.26
  4561.7 36.2 all-reduce.85.cloned.1.call-done
  4681.1 10.6 slice_bitcast_fusion.22
  4711.4 36.2 all-reduce.87.cloned.1.call-done
  4830.8 10.6 slice_bitcast_fusion.18
  4861.1 36.2 all-reduce.89.cloned.1.call-done
  4980.5 10.6 slice_bitcast_fusion.14
  5010.8 36.2 all-reduce.91.cloned.1.call-done
  5130.2 10.6 slice_bitcast_fusion.10
  5160.5 36.2 all-reduce.93.cloned.1.call-done
  5279.9 10.6 slice_bitcast_fusion.6
  5310.2 36.2 all-reduce.95.cloned.1.call-done
  5429.6 10.6 slice_bitcast_fusion.2
  5459.9 36.2 all-reduce.97.cloned.1.call-done
  5543.8 228.7 %all-reduce.99.cloned.1.call-done = (bf16[64,2048]{1,0:T(8,128)(2,1)}, bf16[64,2048]{1,0:T(8,128)(2,1)}, bf16[64,2048]{1,0:T(8,128)(2,1)}, bf16[64,2048]{1,0:T(8...) async-done(((bf16[64,2048]{1,0:T(8,128)(2,1)}, ...) | async-done | bytes 8388624 | tf_op jit(solution)/shard_map/psum | solution.py:84
  (3109 shorter events, 4078.8 us)
Async XLA Ops:
  7.2 830.9 %all-reduce.35.cloned.1.call-start = ((), (), s32[]{:S(2)}) async-start(), calls=%async_computation | async-start | bytes 524288 | tf_op jit(solution)/shard_map/psum | solution.py:84
  40.1 597.6 %copy-start.249 = (f32[64,32]{0,1:T(8,128)}, f32[64,32]{0,1:T(8,128)S(1)}, u32[]{:S(2)}) copy-start(f32[64,32]{0,1:T(8,128)S(1)} %get-tuple-element.806) | copy-start | bytes 24580
  40.1 602.4 %copy-start.245 = (f32[64,32]{0,1:T(8,128)}, f32[64,32]{0,1:T(8,128)S(1)}, u32[]{:S(2)}) copy-start(f32[64,32]{0,1:T(8,128)S(1)} %get-tuple-element.561) | copy-start | bytes 24580
  40.2 602.4 %copy-start.247 = (f32[64,32]{0,1:T(8,128)}, f32[64,32]{0,1:T(8,128)S(1)}, u32[]{:S(2)}) copy-start(f32[64,32]{0,1:T(8,128)S(1)} %get-tuple-element.562) | copy-start | bytes 24580
  95.8 906.3 %all-reduce.37.cloned.1.call-start = ((), (), s32[]{:S(2)}) async-start(), calls=%async_computation.1 | async-start | bytes 524288 | tf_op jit(solution)/shard_map/psum | solution.py:84
  100.0 154.7 %copy-start.522 = (f32[64]{0:T(128)}, f32[64]{0:T(128)S(1)}, u32[]{:S(2)}) copy-start(f32[64]{0:T(128)S(1)} %get-tuple-element.864) | copy-start | bytes 772
  100.0 156.4 %copy-start.524 = (f32[64]{0:T(128)}, f32[64]{0:T(128)S(1)}, u32[]{:S(2)}) copy-start(f32[64]{0:T(128)S(1)} %get-tuple-element.865) | copy-start | bytes 772
  100.0 151.2 %copy-start.518 = (f32[64]{0:T(128)}, f32[64]{0:T(128)S(1)}, u32[]{:S(2)}) copy-start(f32[64]{0:T(128)S(1)} %get-tuple-element.862) | copy-start | bytes 772
  100.0 152.9 %copy-start.520 = (f32[64]{0:T(128)}, f32[64]{0:T(128)S(1)}, u32[]{:S(2)}) copy-start(f32[64]{0:T(128)S(1)} %get-tuple-element.863) | copy-start | bytes 772
  100.1 147.9 %copy-start.514 = (f32[64]{0:T(128)}, f32[64]{0:T(128)S(1)}, u32[]{:S(2)}) copy-start(f32[64]{0:T(128)S(1)} %get-tuple-element.860) | copy-start | bytes 772
  100.1 149.5 %copy-start.516 = (f32[64]{0:T(128)}, f32[64]{0:T(128)S(1)}, u32[]{:S(2)}) copy-start(f32[64]{0:T(128)S(1)} %get-tuple-element.861) | copy-start | bytes 772
  100.1 144.4 %copy-start.510 = (f32[64]{0:T(128)}, f32[64]{0:T(128)S(1)}, u32[]{:S(2)}) copy-start(f32[64]{0:T(128)S(1)} %get-tuple-element.858) | copy-start | bytes 772
  100.1 146.1 %copy-start.512 = (f32[64]{0:T(128)}, f32[64]{0:T(128)S(1)}, u32[]{:S(2)}) copy-start(f32[64]{0:T(128)S(1)} %get-tuple-element.859) | copy-start | bytes 772
  107.7 150.4 %copy-start.526 = (f32[64]{0:T(128)}, f32[64]{0:T(128)S(1)}, u32[]{:S(2)}) copy-start(f32[64]{0:T(128)S(1)} %get-tuple-element.857) | copy-start | bytes 772
  108.3 151.6 %copy-start.528 = (f32[64]{0:T(128)}, f32[64]{0:T(128)S(1)}, u32[]{:S(2)}) copy-start(f32[64]{0:T(128)S(1)} %get-tuple-element.866) | copy-start | bytes 772
  137.1 162.3 %copy-start.317 = (f32[64,2,128]{2,0,1:T(8,128)}, f32[64,2,128]{2,0,1:T(8,128)S(1)}, u32[]{:S(2)}) copy-start(f32[64,2,128]{2,0,1:T(8,128)S(1)} %fusion.3336) | copy-start | bytes 196612
  141.4 158.7 %copy-start.318 = (f32[64,2,128]{2,0,1:T(8,128)}, f32[64,2,128]{2,0,1:T(8,128)S(1)}, u32[]{:S(2)}) copy-start(f32[64,2,128]{2,0,1:T(8,128)S(1)} %fusion.3347) | copy-start | bytes 196612
  145.7 155.2 %copy-start.319 = (f32[64,2,128]{2,0,1:T(8,128)}, f32[64,2,128]{2,0,1:T(8,128)S(1)}, u32[]{:S(2)}) copy-start(f32[64,2,128]{2,0,1:T(8,128)S(1)} %fusion.3358) | copy-start | bytes 196612
  149.9 151.6 %copy-start.320 = (f32[64,2,128]{2,0,1:T(8,128)}, f32[64,2,128]{2,0,1:T(8,128)S(1)}, u32[]{:S(2)}) copy-start(f32[64,2,128]{2,0,1:T(8,128)S(1)} %fusion.3369) | copy-start | bytes 196612
  154.2 148.1 %copy-start.321 = (f32[64,2,128]{2,0,1:T(8,128)}, f32[64,2,128]{2,0,1:T(8,128)S(1)}, u32[]{:S(2)}) copy-start(f32[64,2,128]{2,0,1:T(8,128)S(1)} %fusion.3380) | copy-start | bytes 196612
  158.4 144.5 %copy-start.322 = (f32[64,2,128]{2,0,1:T(8,128)}, f32[64,2,128]{2,0,1:T(8,128)S(1)}, u32[]{:S(2)}) copy-start(f32[64,2,128]{2,0,1:T(8,128)S(1)} %fusion.3391) | copy-start | bytes 196612
  956.5 197.6 %all-reduce.39.cloned.1.call-start = ((), (), s32[]{:S(2)}) async-start(), calls=%async_computation.2 | async-start | bytes 524288 | tf_op jit(solution)/shard_map/psum | solution.py:84
  1112.0 192.5 %all-reduce.41.cloned.1.call-start = ((), (), s32[]{:S(2)}) async-start(), calls=%async_computation.3 | async-start | bytes 524288 | tf_op jit(solution)/shard_map/psum | solution.py:84
  1262.4 192.6 %all-reduce.43.cloned.1.call-start = ((), (), s32[]{:S(2)}) async-start(), calls=%async_computation.4 | async-start | bytes 524288 | tf_op jit(solution)/shard_map/psum | solution.py:84
  1412.9 192.5 %all-reduce.45.cloned.1.call-start = ((), (), s32[]{:S(2)}) async-start(), calls=%async_computation.5 | async-start | bytes 524288 | tf_op jit(solution)/shard_map/psum | solution.py:84
  1563.3 191.8 %all-reduce.47.cloned.1.call-start = ((), (), s32[]{:S(2)}) async-start(), calls=%async_computation.6 | async-start | bytes 524288 | tf_op jit(solution)/shard_map/psum | solution.py:84
  1713.0 191.1 %all-reduce.49.cloned.1.call-start = ((), (), s32[]{:S(2)}) async-start(), calls=%async_computation.7 | async-start | bytes 524288 | tf_op jit(solution)/shard_map/psum | solution.py:84
  1862.0 191.7 %all-reduce.51.cloned.1.call-start = ((), (), s32[]{:S(2)}) async-start(), calls=%async_computation.8 | async-start | bytes 524288 | tf_op jit(solution)/shard_map/psum | solution.py:84
  2011.6 191.7 %all-reduce.53.cloned.1.call-start = ((), (), s32[]{:S(2)}) async-start(), calls=%async_computation.9 | async-start | bytes 524288 | tf_op jit(solution)/shard_map/psum | solution.py:84
  2161.3 191.7 %all-reduce.55.cloned.1.call-start = ((), (), s32[]{:S(2)}) async-start(), calls=%async_computation.10 | async-start | bytes 524288 | tf_op jit(solution)/shard_map/psum | solution.py:84
  2311.0 191.7 %all-reduce.57.cloned.1.call-start = ((), (), s32[]{:S(2)}) async-start(), calls=%async_computation.11 | async-start | bytes 524288 | tf_op jit(solution)/shard_map/psum | solution.py:84
  2460.6 191.8 %all-reduce.59.cloned.1.call-start = ((), (), s32[]{:S(2)}) async-start(), calls=%async_computation.12 | async-start | bytes 524288 | tf_op jit(solution)/shard_map/psum | solution.py:84
  2610.3 191.7 %all-reduce.61.cloned.1.call-start = ((), (), s32[]{:S(2)}) async-start(), calls=%async_computation.13 | async-start | bytes 524288 | tf_op jit(solution)/shard_map/psum | solution.py:84
  2759.9 191.7 %all-reduce.63.cloned.1.call-start = ((), (), s32[]{:S(2)}) async-start(), calls=%async_computation.14 | async-start | bytes 524288 | tf_op jit(solution)/shard_map/psum | solution.py:84
  2909.5 191.7 %all-reduce.65.cloned.1.call-start = ((), (), s32[]{:S(2)}) async-start(), calls=%async_computation.15 | async-start | bytes 524288 | tf_op jit(solution)/shard_map/psum | solution.py:84
  3059.2 191.7 %all-reduce.67.cloned.1.call-start = ((), (), s32[]{:S(2)}) async-start(), calls=%async_computation.16 | async-start | bytes 524288 | tf_op jit(solution)/shard_map/psum | solution.py:84
  3208.8 191.7 %all-reduce.69.cloned.1.call-start = ((), (), s32[]{:S(2)}) async-start(), calls=%async_computation.17 | async-start | bytes 524288 | tf_op jit(solution)/shard_map/psum | solution.py:84
  3358.4 191.7 %all-reduce.71.cloned.1.call-start = ((), (), s32[]{:S(2)}) async-start(), calls=%async_computation.18 | async-start | bytes 524288 | tf_op jit(solution)/shard_map/psum | solution.py:84
  3508.1 191.7 %all-reduce.73.cloned.1.call-start = ((), (), s32[]{:S(2)}) async-start(), calls=%async_computation.19 | async-start | bytes 524288 | tf_op jit(solution)/shard_map/psum | solution.py:84
  3657.7 191.7 %all-reduce.75.cloned.1.call-start = ((), (), s32[]{:S(2)}) async-start(), calls=%async_computation.20 | async-start | bytes 524288 | tf_op jit(solution)/shard_map/psum | solution.py:84
  3807.4 191.8 %all-reduce.77.cloned.1.call-start = ((), (), s32[]{:S(2)}) async-start(), calls=%async_computation.21 | async-start | bytes 524288 | tf_op jit(solution)/shard_map/psum | solution.py:84
  3957.1 191.8 %all-reduce.79.cloned.1.call-start = ((), (), s32[]{:S(2)}) async-start(), calls=%async_computation.22 | async-start | bytes 524288 | tf_op jit(solution)/shard_map/psum | solution.py:84
  4106.8 191.8 %all-reduce.81.cloned.1.call-start = ((), (), s32[]{:S(2)}) async-start(), calls=%async_computation.23 | async-start | bytes 524288 | tf_op jit(solution)/shard_map/psum | solution.py:84
  4256.4 191.8 %all-reduce.83.cloned.1.call-start = ((), (), s32[]{:S(2)}) async-start(), calls=%async_computation.24 | async-start | bytes 524288 | tf_op jit(solution)/shard_map/psum | solution.py:84
  4406.1 191.7 %all-reduce.85.cloned.1.call-start = ((), (), s32[]{:S(2)}) async-start(), calls=%async_computation.25 | async-start | bytes 524288 | tf_op jit(solution)/shard_map/psum | solution.py:84
  4555.8 191.7 %all-reduce.87.cloned.1.call-start = ((), (), s32[]{:S(2)}) async-start(), calls=%async_computation.26 | async-start | bytes 524288 | tf_op jit(solution)/shard_map/psum | solution.py:84
  4705.4 191.8 %all-reduce.89.cloned.1.call-start = ((), (), s32[]{:S(2)}) async-start(), calls=%async_computation.27 | async-start | bytes 524288 | tf_op jit(solution)/shard_map/psum | solution.py:84
  4855.1 191.8 %all-reduce.91.cloned.1.call-start = ((), (), s32[]{:S(2)}) async-start(), calls=%async_computation.28 | async-start | bytes 524288 | tf_op jit(solution)/shard_map/psum | solution.py:84
  5004.8 191.8 %all-reduce.93.cloned.1.call-start = ((), (), s32[]{:S(2)}) async-start(), calls=%async_computation.29 | async-start | bytes 524288 | tf_op jit(solution)/shard_map/psum | solution.py:84
  5154.5 191.9 %all-reduce.95.cloned.1.call-start = ((), (), s32[]{:S(2)}) async-start(), calls=%async_computation.30 | async-start | bytes 524288 | tf_op jit(solution)/shard_map/psum | solution.py:84
  5304.3 191.8 %all-reduce.97.cloned.1.call-start = ((), (), s32[]{:S(2)}) async-start(), calls=%async_computation.31 | async-start | bytes 524288 | tf_op jit(solution)/shard_map/psum | solution.py:84
  5453.9 318.6 %all-reduce.99.cloned.1.call-start = ((), (), s32[]{:S(2)}) async-start(), calls=%async_computation.32 | async-start | bytes 16777216 | tf_op jit(solution)/shard_map/psum | solution.py:84
  5543.7 228.9 %copy-start.1 = (f32[1,2048]{1,0:T(1,128)S(1)}, f32[1,2048]{1,0:T(1,128)}, u32[]{:S(2)}) copy-start(f32[1,2048]{1,0:T(1,128)} %get-tuple-element.551) | copy-start | bytes 24580
  5543.7 228.9 %copy-start.90 = (bf16[64,2048]{1,0:T(8,128)(2,1)S(1)}, bf16[64,2048]{1,0:T(8,128)(2,1)}, u32[]{:S(2)}) copy-start(bf16[64,2048]{1,0:T(8,128)(2,1)} %copy-done.89) | copy-start | bytes 786436
  5543.7 230.1 %copy-start.92 = (bf16[64,2048]{1,0:T(8,128)(2,1)S(1)}, bf16[64,2048]{1,0:T(8,128)(2,1)}, u32[]{:S(2)}) copy-start(bf16[64,2048]{1,0:T(8,128)(2,1)} %copy-done.91) | copy-start | bytes 786436
  5543.7 231.2 %copy-start.94 = (bf16[64,2048]{1,0:T(8,128)(2,1)S(1)}, bf16[64,2048]{1,0:T(8,128)(2,1)}, u32[]{:S(2)}) copy-start(bf16[64,2048]{1,0:T(8,128)(2,1)} %copy-done.93) | copy-start | bytes 786436
  5543.7 232.4 %copy-start.96 = (bf16[64,2048]{1,0:T(8,128)(2,1)S(1)}, bf16[64,2048]{1,0:T(8,128)(2,1)}, u32[]{:S(2)}) copy-start(bf16[64,2048]{1,0:T(8,128)(2,1)} %copy-done.95) | copy-start | bytes 786436
  5543.7 233.5 %copy-start.98 = (bf16[64,2048]{1,0:T(8,128)(2,1)S(1)}, bf16[64,2048]{1,0:T(8,128)(2,1)}, u32[]{:S(2)}) copy-start(bf16[64,2048]{1,0:T(8,128)(2,1)} %copy-done.97) | copy-start | bytes 786436
  5543.7 234.6 %copy-start.100 = (bf16[64,2048]{1,0:T(8,128)(2,1)S(1)}, bf16[64,2048]{1,0:T(8,128)(2,1)}, u32[]{:S(2)}) copy-start(bf16[64,2048]{1,0:T(8,128)(2,1)} %copy-done.99) | copy-start | bytes 786436
  5543.7 235.7 %copy-start.102 = (bf16[64,2048]{1,0:T(8,128)(2,1)S(1)}, bf16[64,2048]{1,0:T(8,128)(2,1)}, u32[]{:S(2)}) copy-start(bf16[64,2048]{1,0:T(8,128)(2,1)} %copy-done.101) | copy-start | bytes 786436
  5543.7 235.8 %copy-start.104 = (bf16[64,2048]{1,0:T(8,128)(2,1)S(1)}, bf16[64,2048]{1,0:T(8,128)(2,1)}, u32[]{:S(2)}) copy-start(bf16[64,2048]{1,0:T(8,128)(2,1)} %copy-done.103) | copy-start | bytes 786436
  5543.8 235.9 %copy-start.106 = (bf16[64,2048]{1,0:T(8,128)(2,1)S(1)}, bf16[64,2048]{1,0:T(8,128)(2,1)}, u32[]{:S(2)}) copy-start(bf16[64,2048]{1,0:T(8,128)(2,1)} %copy-done.105) | copy-start | bytes 786436
  5543.8 236.1 %copy-start.108 = (bf16[64,2048]{1,0:T(8,128)(2,1)S(1)}, bf16[64,2048]{1,0:T(8,128)(2,1)}, u32[]{:S(2)}) copy-start(bf16[64,2048]{1,0:T(8,128)(2,1)} %copy-done.107) | copy-start | bytes 786436
  5543.8 236.2 %copy-start.110 = (bf16[64,2048]{1,0:T(8,128)(2,1)S(1)}, bf16[64,2048]{1,0:T(8,128)(2,1)}, u32[]{:S(2)}) copy-start(bf16[64,2048]{1,0:T(8,128)(2,1)} %copy-done.109) | copy-start | bytes 786436
  (548 other events, 14733.0 us)
Sparse Core Ops, SparseCore 0:
  95.9 45.4 all-reduce.34
  956.6 45.3 all-reduce.36
  1112.1 41.9 all-reduce.38
  1262.5 41.9 all-reduce.40
  1413.0 41.9 all-reduce.42
  1563.4 41.9 all-reduce.44
  1713.1 41.9 all-reduce.46
  1862.1 41.9 all-reduce.48
  2011.8 41.9 all-reduce.50
  2161.4 41.9 all-reduce.52
  2311.1 41.9 all-reduce.54
  2460.7 41.9 all-reduce.56
  2610.4 41.9 all-reduce.58
  2760.0 41.9 all-reduce.60
  2909.6 41.9 all-reduce.62
  3059.3 41.9 all-reduce.64
  3208.9 41.9 all-reduce.66
  3358.5 41.9 all-reduce.68
  3508.2 41.9 all-reduce.70
  3657.8 41.9 all-reduce.72
  3807.5 41.9 all-reduce.74
  3957.2 41.9 all-reduce.76
  4106.9 41.9 all-reduce.78
  4256.6 41.9 all-reduce.80
  4406.2 41.9 all-reduce.82
  4555.9 41.9 all-reduce.84
  4705.5 41.9 all-reduce.86
  4855.2 41.9 all-reduce.88
  5004.9 41.9 all-reduce.90
  5154.6 41.9 all-reduce.92
  5304.4 41.9 all-reduce.94
  5454.1 41.9 all-reduce.96
  5543.9 228.6 all-reduce.98
where the time goes:
time: 5840 us; the launch traced here: 5790 us
  local copies, waits for them, and re-layouts  2840 us (49%)
  waiting for transfers between devices  1350 us (23%)
  matrix products  1170 us (20%)
  other arithmetic  397 us (7%)
    psum x33, waiting for transfers between devices, decode_shard(): layer_sum = lax.psum(layer_part.astype(jnp.bfloat16), 'tp')  1350 us
    squeeze x64, local copies, waits for them, and re-layouts, layer_update(): v_cache[layer_idx]  666 us
    squeeze x64, local copies, waits for them, and re-layouts, layer_update(): k_cache[layer_idx]  656 us
    scatter x64, local copies, waits for them, and re-layouts, layer_update(): k_cache = k_cache.at[layer_idx, batch_rows, new_pos].set(key_new)  581 us
    scatter x64, local copies, waits for them, and re-layouts, layer_update(): v_cache = v_cache.at[layer_idx, batch_rows, new_pos].set(value_new)  564 us
    dot_general x64, matrix products, layer_update(): jnp.dot(gelu_act, out_weight, preferred_element_type=jnp.float32)  381 us
    dot_general x64, matrix products, attend(): jnp.einsum('bhe,bshe->bhs', query, k_layer, preferred_element_type=jnp.fl...  222 us
    dot_general x64, matrix products, attend(): jnp.einsum('bhs,bshe->bhe', attn_probs, v_layer, preferred_element_type=j...  214 us
  transfers between devices with their start and end apart: 33, of which 32 were waited for; matrix products, arithmetic and copies ran while one was open for 16% of the time, Pallas kernels for 0%

commit v1 on v0

v1 whole, which is shorter than its diff:
```python
import jax
import jax.numpy as jnp
from jax import lax
from jax.sharding import PartitionSpec as P

ROT_DIM = 64
LN_EPS = 1e-5
CHUNKS = 2


def layer_norm(hidden, gain, bias):
    hid_f32 = hidden.astype(jnp.float32)
    row_mean = jnp.mean(hid_f32, axis=-1, keepdims=True)
    centered = hid_f32 - row_mean
    row_var = jnp.mean(centered * centered, axis=-1, keepdims=True)
    normed = centered * lax.rsqrt(row_var + LN_EPS)
    return (normed * gain.astype(jnp.float32) + bias.astype(jnp.float32)).astype(jnp.bfloat16)


def rotary_tables(positions):
    lane = jnp.arange(128)
    inv_freq = 1.0 / (10000.0 ** ((lane // 2 * 2).astype(jnp.float32) / ROT_DIM))
    angles = positions.astype(jnp.float32)[..., None] * inv_freq
    inside = lane < ROT_DIM
    cos_tab = jnp.where(inside, jnp.cos(angles), 1.0)
    sin_tab = jnp.where(inside, jnp.where(lane % 2 == 0, -jnp.sin(angles), jnp.sin(angles)), 0.0)
    return cos_tab, sin_tab


def apply_rotary(vectors, cos_tab, sin_tab):
    even_lane = jnp.arange(vectors.shape[-1]) % 2 == 0
    swapped = jnp.where(even_lane, jnp.roll(vectors, -1, axis=-1), jnp.roll(vectors, 1, axis=-1))
    return vectors * cos_tab + swapped * sin_tab


def chunk_layer(hidden, rotary, slot_of, visible, k_cache, v_cache, weights):
    cos_tab, sin_tab = rotary
    gain, bias, q_weight, k_weight, v_weight, o_weight, in_weight, in_bias, out_weight = weights
    steps, n_seq, d_model = hidden.shape
    n_heads, head_dim = k_cache.shape[2:]
    normed = layer_norm(hidden, gain, bias).reshape(steps * n_seq, d_model)
    head_shape = (steps, n_seq, n_heads, head_dim)
    query = jnp.dot(normed, q_weight, preferred_element_type=jnp.float32).reshape(head_shape)
    key_new = jnp.dot(normed, k_weight, preferred_element_type=jnp.float32).reshape(head_shape)
    value_new = jnp.dot(normed, v_weight, preferred_element_type=jnp.float32).astype(jnp.bfloat16).reshape(head_shape)
    query = apply_rotary(query, cos_tab, sin_tab).astype(jnp.bfloat16)
    key_new = apply_rotary(key_new, cos_tab, sin_tab).astype(jnp.bfloat16)
    rows = jnp.arange(n_seq)[None, :]
    k_cache = k_cache.at[rows, slot_of].set(key_new)
    v_cache = v_cache.at[rows, slot_of].set(value_new)
    scores = jnp.einsum("tbhe,bshe->bhts", query, k_cache, preferred_element_type=jnp.float32) * (head_dim ** -0.5)
    scores = jnp.where(visible, scores, -jnp.inf)
    exp_scores = jnp.exp(scores - jnp.max(scores, axis=-1, keepdims=True))
    probs = (exp_scores / jnp.sum(exp_scores, axis=-1, keepdims=True)).astype(jnp.bfloat16)
    context = jnp.einsum("bhts,bshe->tbhe", probs, v_cache, preferred_element_type=jnp.float32).astype(jnp.bfloat16)
    context = context.reshape(steps * n_seq, n_heads * head_dim)
    pre_act = jnp.dot(normed, in_weight, preferred_element_type=jnp.float32) + in_bias.astype(jnp.float32)
    gelu_act = jax.nn.gelu(pre_act, approximate=True).astype(jnp.bfloat16)
    part = jnp.dot(context, o_weight, preferred_element_type=jnp.float32) + jnp.dot(gelu_act, out_weight, preferred_element_type=jnp.float32)
    return part.reshape(hidden.shape), k_cache, v_cache


def decode_shard(x_steps, cur_len, k_cache, v_cache, ln_gain, ln_bias, w_q, w_k, w_v, w_o, w_in, b_in, w_out, b_out):
    n_layers, batch, cache_len = k_cache.shape[:3]
    steps = x_steps.shape[0]
    size = batch // CHUNKS
    hiddens, k_parts, v_parts = [], [], []
    for chunk in range(CHUNKS):
        part = slice(chunk * size, (chunk + 1) * size)
        lens = cur_len[part]
        slot_of = lens[None, :] + jnp.arange(steps)[:, None]
        cos_tab, sin_tab = rotary_tables(slot_of)
        rotary = (cos_tab[:, :, None, :], sin_tab[:, :, None, :])
        visible = (jnp.arange(cache_len)[None, None, :] <= slot_of.T[:, :, None])[:, None]
        hidden = x_steps[:, part]
        ks, vs = [], []
        for layer in range(n_layers):
            weights = (ln_gain[layer], ln_bias[layer], w_q[layer], w_k[layer], w_v[layer], w_o[layer], w_in[layer], b_in[layer], w_out[layer])
            update, k_new, v_new = chunk_layer(hidden, rotary, slot_of, visible, k_cache[layer, part], v_cache[layer, part], weights)
            total = lax.psum(update.astype(jnp.bfloat16), "tp")
            hidden = (hidden.astype(jnp.float32) + total.astype(jnp.float32) + b_out[layer].astype(jnp.float32)).astype(jnp.bfloat16)
            ks.append(k_new)
            vs.append(v_new)
        hiddens.append(hidden)
        k_parts.append(jnp.stack(ks))
        v_parts.append(jnp.stack(vs))
    return jnp.concatenate(hiddens, axis=1), jnp.concatenate(k_parts, axis=1), jnp.concatenate(v_parts, axis=1)


def solution(mesh):
    cache_spec = P(None, "dp", None, "tp", None)
    in_specs = (P(None, "dp", None), P("dp"), cache_spec, cache_spec, P(None, None), P(None, None),
                P(None, None, "tp"), P(None, None, "tp"), P(None, None, "tp"), P(None, "tp", None),
                P(None, None, "tp"), P(None, "tp"), P(None, "tp", None), P(None, None))
    out_specs = (P(None, "dp", None), cache_spec, cache_spec)
    return jax.shard_map(decode_shard, mesh=mesh, in_specs=in_specs, out_specs=out_specs, check_vma=False)
```

time: 5840 us -> 1110 us (0.19)
  local copies, waits for them, and re-layouts: 2840 us -> 628 us
  waiting for transfers between devices: 1350 us -> 198 us
  matrix products: 1170 us -> 155 us
  other arithmetic: 397 us -> 106 us
    squeeze x128 -> x0, local copies, waits for them, and re-layouts: 1320 us -> none  [the longest x64 666 us: layer_update(): v_cache[layer_idx]]
    psum x33 -> x2, waiting for transfers between devices: 1350 us -> 197 us  [decode_shard(): total = lax.psum(update.astype(jnp.bfloat16), 'tp')]
    scatter x128 -> x0, local copies, waits for them, and re-layouts: 1140 us -> none  [the longest x64 581 us: layer_update(): k_cache = k_cache.at[layer_idx, batch_rows, new_pos].set(key_new)]
    dot_general x448 -> x28, matrix products: 1170 us -> 155 us  [the longest x4 70.1 us: chunk_layer(): jnp.dot(gelu_act, out_weight, preferred_element_type=jnp.float32)]
    unnamed x1160 -> x126, local copies, waits for them, and re-layouts: 21.4 us -> 559 us
    another operation x193 -> x0, other arithmetic: 127 us -> none  [the longest x128 67.6 us: apply_rotary(): jnp.stack([even_part * cos_tab - odd_part * sin_tab, odd_part * cos_tab +...]
    reshape x192 -> x4, local copies, waits for them, and re-layouts: 132 us -> 8.64 us  [chunk_layer(): jnp.dot(normed, v_weight, preferred_element_type=jnp.float32)]
    slice x256 -> x19, local copies, waits for them, and re-layouts: 169 us -> 46.6 us  [the longest x16 27.3 us: apply_rotary(): jnp.roll(vectors, 1, axis=-1)]
  transfers between devices with their start and end apart: 33 -> 2, of which waited for: 32 -> 2; matrix products, arithmetic and copies ran while one was open for 16% -> 3% of each run, Pallas kernels for 0% -> 0%
where the time goes in v1:
time: 1110 us; the launch traced here: 1100 us
  local copies, waits for them, and re-layouts  628 us (57%)
  waiting for transfers between devices  198 us (18%)
  matrix products  155 us (14%)
  other arithmetic  106 us (10%)
  between operations  15.4 us (1%)
    unnamed x126, local copies, waits for them, and re-layouts  559 us
    psum x2, waiting for transfers between devices, decode_shard(): total = lax.psum(update.astype(jnp.bfloat16), 'tp')  197 us
    dot_general x4, matrix products, chunk_layer(): jnp.dot(gelu_act, out_weight, preferred_element_type=jnp.float32)  70.1 us
    dot_general x4, matrix products, chunk_layer(): jnp.dot(context, o_weight, preferred_element_type=jnp.float32)  27.4 us
    slice x16, local copies, waits for them, and re-layouts, apply_rotary(): jnp.roll(vectors, 1, axis=-1)  27.3 us
    dot_general x4, matrix products, chunk_layer(): jnp.einsum('bhts,bshe->tbhe', probs, v_cache, preferred_element_type=jnp....  25.4 us
  transfers between devices with their start and end apart: 2, of which 2 were waited for; matrix products, arithmetic and copies ran while one was open for 3% of the time, Pallas kernels for 0%

profile of v1, /device:TPU:0, one launch (start us, length us, event | category | flops | bytes accessed | tf_op | source)
XLA Modules:
  0.0 1101.8 jit_solution(1243607437011576156)
XLA Ops:
  9.7 4.3 convert_reduce_fusion.3
  15.6 2.5 fusion.24
  22.4 5.9 fusion.27
  34.2 1.7 fusion.323
  37.6 1.7 fusion.319
  39.3 1.7 fusion.318
  44.4 1.7 fusion.321
  46.1 1.8 fusion.320
  48.0 2.1 convolution_convert_fusion.1
  50.1 2.1 convolution_convert_fusion.3
  52.2 17.7 %fusion.88 = f32[1024,2048]{1,0:T(8,128)} fusion(bf16[2,1024,2048]{2,1,0:T(8,128)(2,1)} %param.26, f32[1024]{0:T(1024)S(1)} %bitcast.286, bf16[1024,2048]{1,0:T(8,128)(2,1)} %bitcast.253, bf16[2,2048,1024]{2,1,0:T(8,128)(2,1)} %param.24), kind=kOutput, calls=%fused_computation.119 | convolution fusion | flops 8600420352 | bytes 20975616 | tf_op jit(solution)/shard_map/dot_general | solution.py:59
  69.9 17.4 %fusion.90 = f32[1024,2048]{1,0:T(8,128)} fusion(bf16[2,1024,2048]{2,1,0:T(8,128)(2,1)} %param.26, f32[1024]{0:T(1024)S(1)} %bitcast.287, bf16[1024,2048]{1,0:T(8,128)(2,1)} %bitcast.251, bf16[2,2048,1024]{2,1,0:T(8,128)(2,1)} %param.24), kind=kOutput, calls=%fused_computation.121 | convolution fusion | flops 8600420352 | bytes 20975616 | tf_op jit(solution)/shard_map/dot_general | solution.py:59
  88.1 2.0 copy.127
  90.1 2.4 copy.105
  92.5 3.8 fusion.245
  96.5 6.8 fusion.218
  104.0 2.3 fusion.206
  107.0 8.0 fusion.308
  115.0 93.4 %scatter_fusion.1 = bf16[4096,2,128]{2,1,0:T(2,128)(2,1)} fusion(bf16[4096,2,128]{2,1,0:T(2,128)(2,1)} %bitcast.242, s32[1024]{0:T(1024)S(1)} %reshape.431, bf16[1024,2,128]{2,1,0:T(2,128)(2,1)S(1)} %copy.110), kind=kCustom, calls=%fused_computation.1 | custom fusion | bytes 1576960
  208.4 3.0 fusion.159
  212.3 27.9 %scatter_fusion.5 = bf16[4096,2,128]{2,1,0:T(2,128)(2,1)S(1)} fusion(bf16[4096,2,128]{2,1,0:T(2,128)(2,1)S(1)} %bitcast.239, s32[1024]{0:T(1024)S(1)} %reshape.455, bf16[1024,2,128]{2,1,0:T(2,128)(2,1)S(1)} %copy.130), kind=kCustom, calls=%fused_computation.5 | custom fusion | bytes 1576960
  240.2 2.6 fusion.171
  244.5 10.5 fusion.309
  255.0 93.2 %scatter_fusion = bf16[4096,2,128]{2,1,0:T(2,128)(2,1)} fusion(bf16[4096,2,128]{2,1,0:T(2,128)(2,1)} %bitcast.245, s32[1024]{0:T(1024)S(1)} %reshape.431, bf16[1024,2,128]{2,1,0:T(2,128)(2,1)S(1)} %copy-done.38), kind=kCustom, calls=%fused_computation | custom fusion | bytes 1576960
  348.2 6.8 fusion.201
  356.6 27.9 %scatter_fusion.4 = bf16[4096,2,128]{2,1,0:T(2,128)(2,1)S(1)} fusion(bf16[4096,2,128]{2,1,0:T(2,128)(2,1)S(1)} %bitcast.236, s32[1024]{0:T(1024)S(1)} %reshape.455, bf16[1024,2,128]{2,1,0:T(2,128)(2,1)S(1)} %copy-done.37), kind=kCustom, calls=%fused_computation.4 | custom fusion | bytes 1576960
  384.5 5.9 fusion.195
  391.0 7.1 add_convert_fusion.3
  398.1 6.7 add_convert_fusion.1
  408.1 114.3 %all-reduce.7.cloned.1.call-done = (bf16[32,32,2048]{2,1,0:T(8,128)(2,1)}, bf16[32,32,2048]{2,1,0:T(8,128)(2,1)}) async-done(((bf16[32,32,2048]{2,1,0:T(8,128)(2,1)}, bf16[32,32,2048]{2,1,0:T(8,128)(2,1)}), (bf16[32,32,2048]{2,1,0:T(8,128)(2,1)}, bf16[32,32,2048]{2,1,0:T(8,128)(2,1)})) %all-reduce.7.cloned.1.call-update) | async-done | bytes 8388624 | tf_op jit(solution)/shard_map/psum | solution.py:80
  522.5 7.5 convert_reduce_fusion.2
  533.3 3.8 fusion.23
  538.5 3.3 fusion.68
  544.4 1.7 fusion.315
  546.1 1.7 fusion.314
  547.8 1.7 fusion.311
  549.5 1.7 fusion.310
  552.9 1.7 fusion.316
  554.6 1.7 fusion.313
  556.4 1.7 fusion.312
  558.1 2.1 convolution_convert_fusion
  560.2 2.1 convolution_convert_fusion.2
  562.3 17.6 %fusion.76 = f32[1024,2048]{1,0:T(8,128)} fusion(bf16[2,1024,2048]{2,1,0:T(8,128)(2,1)} %param.26, f32[1024]{0:T(1024)S(1)} %bitcast.284, bf16[1024,2048]{1,0:T(8,128)(2,1)} %bitcast.257, bf16[2,2048,1024]{2,1,0:T(8,128)(2,1)} %param.24), kind=kOutput, calls=%fused_computation.107 | convolution fusion | flops 8600420352 | bytes 20975616 | tf_op jit(solution)/shard_map/dot_general | solution.py:59
  579.9 17.4 %fusion.78 = f32[1024,2048]{1,0:T(8,128)} fusion(bf16[2,1024,2048]{2,1,0:T(8,128)(2,1)} %param.26, f32[1024]{0:T(1024)S(1)} %bitcast.285, bf16[1024,2048]{1,0:T(8,128)(2,1)} %bitcast.255, bf16[2,2048,1024]{2,1,0:T(8,128)(2,1)} %param.24), kind=kOutput, calls=%fused_computation.109 | convolution fusion | flops 8600420352 | bytes 20975616 | tf_op jit(solution)/shard_map/dot_general | solution.py:59
  597.3 2.0 copy.136
  599.3 2.2 copy.116
  601.5 6.3 fusion.224
  608.5 93.1 %scatter_fusion.7 = bf16[4096,2,128]{2,1,0:T(2,128)(2,1)} fusion(bf16[4096,2,128]{2,1,0:T(2,128)(2,1)} %bitcast.230, s32[1024]{0:T(1024)S(1)} %reshape.455, bf16[1024,2,128]{2,1,0:T(2,128)(2,1)S(1)} %copy.139), kind=kCustom, calls=%fused_computation.7 | custom fusion | bytes 1576960
  701.5 3.0 fusion.177
  706.1 93.2 %scatter_fusion.6 = bf16[4096,2,128]{2,1,0:T(2,128)(2,1)} fusion(bf16[4096,2,128]{2,1,0:T(2,128)(2,1)} %bitcast.233, s32[1024]{0:T(1024)S(1)} %reshape.455, bf16[1024,2,128]{2,1,0:T(2,128)(2,1)S(1)} %copy-done.40), kind=kCustom, calls=%fused_computation.6 | custom fusion | bytes 1576960
  799.4 6.7 fusion.192
  806.1 2.4 copy.144
  808.5 5.7 fusion.212
  814.8 93.3 %scatter_fusion.3 = bf16[4096,2,128]{2,1,0:T(2,128)(2,1)} fusion(bf16[4096,2,128]{2,1,0:T(2,128)(2,1)} %bitcast.224, s32[1024]{0:T(1024)S(1)} %reshape.431, bf16[1024,2,128]{2,1,0:T(2,128)(2,1)S(1)} %copy.121), kind=kCustom, calls=%fused_computation.3 | custom fusion | bytes 1576960
  908.1 3.0 fusion.165
  912.1 28.1 %scatter_fusion.2 = bf16[4096,2,128]{2,1,0:T(2,128)(2,1)S(1)} fusion(bf16[4096,2,128]{2,1,0:T(2,128)(2,1)S(1)} %bitcast.227, s32[1024]{0:T(1024)S(1)} %reshape.431, bf16[1024,2,128]{2,1,0:T(2,128)(2,1)S(1)} %copy-done.39), kind=kCustom, calls=%fused_computation.2 | custom fusion | bytes 1576960
  940.2 5.9 fusion.198
  946.8 7.0 add_convert_fusion
  953.8 6.6 add_convert_fusion.2
  962.0 15.6 %maximum_maximum_fusion = bf16[2,64,128,2,128]{4,3,2,1,0:T(2,128)(2,1)} fusion(bf16[1,32,128,2,128]{4,3,2,1,0:T(2,128)(2,1)} %bitcast.232, bf16[1,32,128,2,128]{4,3,2,1,0:T(2,128)(2,1)} %bitcast.241, bf16[1,32,128,2,128]{4,3,2,1,0:T(2,128)(2,1)S(1)} %bitcast.226, bf16[1,32,128,2,128]{4,3,2,1,0:T(2,128)(2,1)} %bitcast.244), kind=kLoop, calls=%fused_computation.57 | loop fusion | flops 12582912 | bytes 16777216 | tf_op jit(solution)/shard_map/concatenate | solution.py:87
  977.6 14.6 %maximum_maximum_fusion.1 = bf16[2,64,128,2,128]{4,3,2,1,0:T(2,128)(2,1)} fusion(bf16[1,32,128,2,128]{4,3,2,1,0:T(2,128)(2,1)S(1)} %bitcast.235, bf16[1,32,128,2,128]{4,3,2,1,0:T(2,128)(2,1)S(1)} %bitcast.238, bf16[1,32,128,2,128]{4,3,2,1,0:T(2,128)(2,1)S(1)} %bitcast.229, bf16[1,32,128,2,128]{4,3,2,1,0:T(2,128)(2,1)S(1)} %bitcast.247), kind=kLoop, calls=%fused_computation.58 | loop fusion | flops 12582912 | bytes 16777216 | tf_op jit(solution)/shard_map/concatenate | solution.py:87
  992.2 83.1 %all-reduce.5.cloned.1.call-done = (bf16[32,32,2048]{2,1,0:T(8,128)(2,1)}, bf16[32,32,2048]{2,1,0:T(8,128)(2,1)}) async-done(((bf16[32,32,2048]{2,1,0:T(8,128)(2,1)}, bf16[32,32,2048]{2,1,0:T(8,128)(2,1)}), (bf16[32,32,2048]{2,1,0:T(8,128)(2,1)}, bf16[32,32,2048]{2,1,0:T(8,128)(2,1)})) %all-reduce.5.cloned.1.call-update) | async-done | bytes 8388624 | tf_op jit(solution)/shard_map/psum | solution.py:80
  1075.3 10.7 fusion.31
  1086.0 8.5 pad_maximum_fusion
  (180 shorter events, 44.2 us)
Async XLA Ops:
  7.2 515.3 %all-reduce.7.cloned.1.call-start = ((), (), s32[]{:S(2)}) async-start(), calls=%async_computation.1 | async-start | bytes 16777216 | tf_op jit(solution)/shard_map/psum | solution.py:80
  9.7 5.9 copy-start
  15.6 2.5 copy-start.41
  18.0 2.6 copy-start.42
  28.3 19.6 %copy-start.23 = (bf16[32,32,2048]{2,1,0:T(8,128)(2,1)}, bf16[32,32,2048]{2,1,0:T(8,128)(2,1)S(1)}, u32[]{:S(2)}) copy-start(bf16[32,32,2048]{2,1,0:T(8,128)(2,1)S(1)} %get-tuple-element.20) | copy-start | bytes 12582916
  28.3 21.7 %copy-start.22 = (bf16[32,32,2048]{2,1,0:T(8,128)(2,1)}, bf16[32,32,2048]{2,1,0:T(8,128)(2,1)S(1)}, u32[]{:S(2)}) copy-start(bf16[32,32,2048]{2,1,0:T(8,128)(2,1)S(1)} %get-tuple-element.19) | copy-start | bytes 12582916
  29.6 2.0 copy-start.45
  34.2 3.4 copy-start.3
  44.4 3.5 copy-start.51
  44.4 3.6 copy-start.54
  69.9 17.4 %copy-start.52 = (s32[2]{0:T(128)S(1)}, s32[2]{0:T(128)}, u32[]{:S(2)}) copy-start(s32[2]{0:T(128)} %constant.106) | copy-start | bytes 28
  69.9 17.5 %copy-start.53 = (s32[2]{0:T(128)S(1)}, s32[2]{0:T(128)}, u32[]{:S(2)}) copy-start(s32[2]{0:T(128)} %constant.103) | copy-start | bytes 28
  96.3 7.0 copy-start.20
  96.4 7.0 copy-start.21
  96.4 7.6 copy-start.16
  96.4 7.6 copy-start.18
  96.4 7.6 copy-start.26
  96.4 7.6 copy-start.27
  96.4 7.6 copy-start.28
  96.4 7.6 copy-start.29
  96.4 7.6 copy-start.30
  96.4 7.6 copy-start.31
  96.4 7.6 copy-start.32
  96.5 7.6 copy-start.33
  96.5 10.5 slice-start
  103.9 3.1 slice-start.1
  211.3 1.0 copy-start.47
  240.2 2.6 copy-start.12
  242.8 1.0 copy-start.46
  244.5 10.5 copy-start.38
  348.2 8.4 copy-start.37
  384.5 13.6 %copy-start.10 = (bf16[4096,2,128]{2,1,0:T(2,128)(2,1)}, bf16[4096,2,128]{2,1,0:T(2,128)(2,1)S(1)}, u32[]{:S(2)}) copy-start(bf16[4096,2,128]{2,1,0:T(2,128)(2,1)S(1)} %scatter_fusion.4) | copy-start | bytes 6291460
  391.0 7.1 copy-start.14
  404.8 1.2 copy-start.34
  404.8 2.6 copy-start.35
  404.8 3.3 copy-start.50
  404.8 670.5 %all-reduce.5.cloned.1.call-start = ((), (), s32[]{:S(2)}) async-start(), calls=%async_computation | async-start | bytes 16777216 | tf_op jit(solution)/shard_map/psum | solution.py:80
  408.1 129.0 %copy-start.44 = (bf16[256,2048]{1,0:T(8,128)(2,1)}, bf16[256,2048]{1,0:T(8,128)(2,1)S(1)}, u32[]{:S(2)}) copy-start(bf16[256,2048]{1,0:T(8,128)(2,1)S(1)} %copy.119) | copy-start | bytes 3145732
  530.0 2.6 copy-start.1
  530.0 3.3 copy-start.2
  537.1 21.0 %copy-start.25 = (bf16[32,32,2048]{2,1,0:T(8,128)(2,1)}, bf16[32,32,2048]{2,1,0:T(8,128)(2,1)S(1)}, u32[]{:S(2)}) copy-start(bf16[32,32,2048]{2,1,0:T(8,128)(2,1)S(1)} %get-tuple-element.80) | copy-start | bytes 12582916
  537.1 23.1 %copy-start.24 = (bf16[32,32,2048]{2,1,0:T(8,128)(2,1)}, bf16[32,32,2048]{2,1,0:T(8,128)(2,1)S(1)}, u32[]{:S(2)}) copy-start(bf16[32,32,2048]{2,1,0:T(8,128)(2,1)S(1)} %get-tuple-element.79) | copy-start | bytes 12582916
  538.4 3.4 copy-start.43
  544.4 3.4 copy-start.4
  554.6 3.4 copy-start.55
  607.9 98.3 %copy-start.40 = (bf16[1024,2,128]{2,1,0:T(2,128)(2,1)S(1)}, bf16[1024,2,128]{2,1,0:T(2,128)(2,1)}, u32[]{:S(2)}) copy-start(bf16[1024,2,128]{2,1,0:T(2,128)(2,1)} %copy.136) | copy-start | bytes 1572868
  704.5 1.0 copy-start.49
  799.4 9.2 copy-start.17
  799.4 9.2 copy-start.19
  814.3 97.8 %copy-start.6 = (bf16[1,32,128,2,128]{4,3,2,1,0:T(2,128)(2,1)S(1)}, bf16[1,32,128,2,128]{4,3,2,1,0:T(2,128)(2,1)}, u32[]{:S(2)}) copy-start(bf16[1,32,128,2,128]{4,3,2,1,0:T(2,128)(2,1)} %get-tuple-element.27) | copy-start | bytes 6291460
  814.3 97.8 %copy-start.39 = (bf16[1024,2,128]{2,1,0:T(2,128)(2,1)S(1)}, bf16[1024,2,128]{2,1,0:T(2,128)(2,1)}, u32[]{:S(2)}) copy-start(bf16[1024,2,128]{2,1,0:T(2,128)(2,1)} %copy.116) | copy-start | bytes 1572868
  911.1 1.0 copy-start.48
  940.2 13.6 %copy-start.7 = (bf16[4096,2,128]{2,1,0:T(2,128)(2,1)}, bf16[4096,2,128]{2,1,0:T(2,128)(2,1)S(1)}, u32[]{:S(2)}) copy-start(bf16[4096,2,128]{2,1,0:T(2,128)(2,1)S(1)} %scatter_fusion.2) | copy-start | bytes 6291460
  940.2 6.5 copy-start.36
  946.7 7.0 copy-start.15
  960.4 1.6 copy-start.5
  962.0 15.6 %copy-start.8 = (bf16[4096,2,128]{2,1,0:T(2,128)(2,1)S(1)}, bf16[4096,2,128]{2,1,0:T(2,128)(2,1)}, u32[]{:S(2)}) copy-start(bf16[4096,2,128]{2,1,0:T(2,128)(2,1)} %copy-done.7) | copy-start | bytes 6291460
  962.0 15.6 %copy-start.9 = (bf16[4096,2,128]{2,1,0:T(2,128)(2,1)S(1)}, bf16[4096,2,128]{2,1,0:T(2,128)(2,1)}, u32[]{:S(2)}) copy-start(bf16[4096,2,128]{2,1,0:T(2,128)(2,1)} %scatter_fusion.6) | copy-start | bytes 6291460
  962.0 15.6 %copy-start.11 = (bf16[4096,2,128]{2,1,0:T(2,128)(2,1)S(1)}, bf16[4096,2,128]{2,1,0:T(2,128)(2,1)}, u32[]{:S(2)}) copy-start(bf16[4096,2,128]{2,1,0:T(2,128)(2,1)} %copy-done.10) | copy-start | bytes 6291460
  962.0 15.6 %copy-start.13 = (bf16[4096,2,128]{2,1,0:T(2,128)(2,1)S(1)}, bf16[4096,2,128]{2,1,0:T(2,128)(2,1)}, u32[]{:S(2)}) copy-start(bf16[4096,2,128]{2,1,0:T(2,128)(2,1)} %scatter_fusion) | copy-start | bytes 6291460
Sparse Core Ops, SparseCore 0:
  404.9 117.4 all-reduce.6
  960.6 114.7 all-reduce.4

commit v2 on v0

v2 whole, which is shorter than its diff:
```python
import functools

import jax
import jax.numpy as jnp
from jax import lax
from jax.experimental import pallas as pl
from jax.experimental.pallas import tpu as pltpu
from jax.sharding import PartitionSpec as P

ROT_DIM = 64
LN_EPS = 1e-5
MESH = pl.DeviceIdType.MESH
F32 = jnp.float32
BF16 = jnp.bfloat16
SEQS = 8
OLD = 96


def decode_kernel(n_chunks, n_stages, x_hbm, k_hbm, v_hbm, wq_hbm, wk_hbm, wv_hbm, wo_hbm, win_hbm, wout_hbm,
                  cos_c, sin_c, cos_t, sin_t, old_mask, gain, bias, b_in, b_out,
                  out_hbm, rec_k, rec_v,
                  wq, wk, wv, wo, win, wout, hid, part, recv0, sum0, recv1, sum1, recv2,
                  normed, qf, kf, vf, cf, ctx, act, inter, scores, kbuf, vbuf,
                  w_sem, x_sem, kv_sem, rec_sem, out_sem, send_sem, recv_sem):
    steps = x_hbm.shape[0]
    rows = steps * SEQS
    half, quarter, eighth = steps // 2, steps // 4, steps // 8
    d_model = x_hbm.shape[2]
    me = lax.axis_index("tp")
    core = lax.rem(me, 2)
    px = lax.rem(lax.div(me, 2), 2)
    py = lax.div(me, 4)
    partner = me + 1 - 2 * core
    x_peer = me + 2 * (1 - 2 * px)
    y_peer = me + 4 * (1 - 2 * py)
    first = (1 - core) * x_peer + core * y_peer
    second = (1 - core) * y_peer + core * x_peer
    pos1 = (1 - core) * px + core * py
    pos2 = (1 - core) * py + core * px
    base0 = half * core
    base1 = base0 + quarter * pos1
    base2 = base1 + eighth * pos2

    weight_pairs = ((wq_hbm, wq), (wk_hbm, wk), (wv_hbm, wv), (win_hbm, win), (wo_hbm, wo), (wout_hbm, wout))

    def weight_copy(layer, j):
        src, dst = weight_pairs[j]
        return pltpu.make_async_copy(src.at[layer], dst.at[layer], w_sem.at[layer, j])

    def x_copy(chunk):
        return pltpu.make_async_copy(x_hbm.at[:, pl.ds(pl.multiple_of(chunk * SEQS, SEQS), SEQS), :], hid.at[chunk], x_sem.at[chunk])

    def out_copy(chunk):
        return pltpu.make_async_copy(hid.at[chunk], out_hbm.at[:, pl.ds(pl.multiple_of(chunk * SEQS, SEQS), SEQS), :], out_sem.at[chunk])

    def kv_copies(stage):
        layer, chunk, slot = lax.div(stage, n_chunks), lax.rem(stage, n_chunks), lax.rem(stage, 2)
        seqs = pl.ds(chunk * SEQS, SEQS)
        return (pltpu.make_async_copy(k_hbm.at[layer, seqs], kbuf.at[slot], kv_sem.at[0, slot]),
                pltpu.make_async_copy(v_hbm.at[layer, seqs], vbuf.at[slot], kv_sem.at[1, slot]))

    def rec_copies(stage):
        layer, chunk, slot = lax.div(stage, n_chunks), lax.rem(stage, n_chunks), lax.rem(stage, 2)
        seqs = pl.ds(chunk * SEQS, SEQS)
        new = pl.ds(2 * OLD, 2 * steps)
        return (pltpu.make_async_copy(kbuf.at[slot, :, new, :], rec_k.at[layer, seqs], rec_sem.at[0, slot]),
                pltpu.make_async_copy(vbuf.at[slot, :, new, :], rec_v.at[layer, seqs], rec_sem.at[1, slot]))

    def remote(phase, stage, src, dst, peer):
        slot = lax.rem(stage, 2)
        return pltpu.make_async_remote_copy(src_ref=src, dst_ref=dst, send_sem=send_sem.at[phase, slot], recv_sem=recv_sem.at[phase, lax.rem(stage, 4)],
                                            device_id={"tp": peer}, device_id_type=MESH)

    def phase0(stage):
        return remote(0, stage, part.at[pl.ds(half - base0, half)], recv0.at[lax.rem(stage, 2)], partner)

    def phase1(stage):
        return remote(1, stage, sum0.at[pl.ds(quarter * (1 - pos1), quarter)], recv1.at[lax.rem(stage, 2)], first)

    def phase2(stage):
        return remote(2, stage, sum1.at[pl.ds(eighth * (1 - pos2), eighth)], recv2.at[lax.rem(stage, 2)], second)

    def gather(phase, stage, start, size, peer):
        block = hid.at[lax.rem(stage, n_chunks), pl.ds(start, size)]
        return remote(phase, stage, block, block, peer)

    def phase3(stage):
        return gather(3, stage, base2, eighth, second)

    def phase4(stage):
        return gather(4, stage, base1, quarter, first)

    def phase5(stage):
        return gather(5, stage, base0, half, partner)

    barrier = pltpu.get_barrier_semaphore()
    for peer in (partner, x_peer, y_peer):
        pl.semaphore_signal(barrier, inc=1, device_id={"tp": peer}, device_id_type=MESH)
    x_copy(0).start()
    for j in range(3):
        weight_copy(0, j).start()
    for copy in kv_copies(0):
        copy.start()
    for j in range(3, 6):
        weight_copy(0, j).start()
    for chunk in range(1, n_chunks):
        x_copy(chunk).start()
    for j in range(6):
        weight_copy(1, j).start()
    pl.semaphore_wait(barrier, 3)

    def norm_and_project(stage, layer, chunk):
        @pl.when(layer == 0)
        def _():
            x_copy(chunk).wait()

        group = 8

        @pl.loop(0, steps // group)
        def _(g):
            x = hid[chunk, pl.ds(g * group, group)].astype(F32)
            mean = jnp.mean(x, axis=-1, keepdims=True)
            centered = x - mean
            var = jnp.mean(centered * centered, axis=-1, keepdims=True)
            y = centered * lax.rsqrt(var + LN_EPS) * gain[layer][None] + bias[layer][None]
            normed[pl.ds(pl.multiple_of(g * group * SEQS, group * SEQS), group * SEQS), :] = y.reshape(group * SEQS, d_model).astype(BF16)

        @pl.when(chunk == 0)
        def _():
            for j in range(3):
                weight_copy(layer, j).wait()

        here = pl.ds(pl.multiple_of(chunk * SEQS, SEQS), SEQS)
        cc, sc = cos_c[here, :][None], sin_c[here, :][None]
        ct, st = cos_t[...], sin_t[...]
        cos = (cc * ct - sc * st).reshape(rows, 128)
        sin = (sc * ct + cc * st).reshape(rows, 128)
        even = lax.rem(lax.broadcasted_iota(jnp.int32, (rows, 128), 1), 2) == 0

        for weight, dst, rotate in ((wq, qf, True), (wk, kf, True), (wv, vf, False)):
            vec = jnp.dot(normed[...], weight[layer], preferred_element_type=F32)
            for h in range(2):
                piece = vec[:, h * 128:(h + 1) * 128]
                if rotate:
                    swapped = jnp.where(even, pltpu.roll(piece, 127, 1), pltpu.roll(piece, 1, 1))
                    piece = piece * cos + swapped * sin
                dst[h] = piece

    def attend(stage, layer, chunk):
        slot = lax.rem(stage, 2)
        for copy in kv_copies(stage):
            copy.wait()
        shape = (2 * steps, 2 * (OLD + steps))
        row, col = lax.broadcasted_iota(jnp.int32, shape, 0), lax.broadcasted_iota(jnp.int32, shape, 1)
        col_slot, col_head = lax.shift_right_logical(col, 1), lax.bitwise_and(col, 1)
        row_head, row_step = lax.div(row, steps), lax.rem(row, steps)
        same = row_head == col_head
        fresh = jnp.where(col_slot - OLD <= row_step, 2.0, 0.0)
        kind = jnp.where(same, jnp.where(col_slot >= OLD, fresh, 1.0), 0.0)
        here = pl.ds(pl.multiple_of(chunk * SEQS, SEQS), SEQS)
        old = old_mask[here, :]
        for b in range(SEQS):
            mine = pl.ds(b, steps, stride=SEQS)
            for src, buf, j in ((kf, kbuf, 0), (vf, vbuf, 1)):
                for h in range(2):
                    inter[b, j, pl.ds(h, steps, stride=2), :] = src[h, mine, :]
                buf[slot, b, pl.ds(2 * OLD, 2 * steps), :] = inter[b, j].astype(BF16)
        for copy in rec_copies(stage):
            copy.start()
        for b in range(SEQS):
            mine = pl.ds(b, steps, stride=SEQS)
            query = jnp.concatenate([qf[0, mine, :], qf[1, mine, :]], axis=0).astype(BF16)
            s = lax.dot_general(query, kbuf[slot, b], (((1,), (1,)), ((), ())), preferred_element_type=F32) * (128 ** -0.5)
            scores[b] = jnp.where(kind + old[b:b + 1, :] > 1.5, s, -jnp.inf)
        for b in range(SEQS):
            s = scores[b]
            e = jnp.exp(s - jnp.max(s, axis=-1, keepdims=True))
            probs = (e * (1.0 / jnp.sum(e, axis=-1, keepdims=True))).astype(BF16)
            context = jnp.dot(probs, vbuf[slot, b], preferred_element_type=F32)
            for h in range(2):
                cf[h, pl.ds(b, steps, stride=SEQS), :] = context[h * steps:(h + 1) * steps]

    def feed_forward(layer, chunk):
        @pl.when(chunk == 0)
        def _():
            for j in range(3, 6):
                weight_copy(layer, j).wait()

        @pl.loop(0, act.shape[1] // 256)
        def _(n):
            cols = pl.ds(pl.multiple_of(n * 256, 256), 256)
            pre = jnp.dot(normed[...], win[layer, :, cols], preferred_element_type=F32) + b_in[layer, :, cols]
            act[:, cols] = jax.nn.gelu(pre, approximate=True).astype(BF16)

    def project_out(stage, layer):
        for h in range(2):
            ctx[:, h * 128:(h + 1) * 128] = cf[h].astype(BF16)

        @pl.loop(0, d_model // 256)
        def _(n):
            cols = pl.ds(pl.multiple_of(n * 256, 256), 256)
            total = jnp.dot(ctx[...], wo[layer, :, cols], preferred_element_type=F32)
            total += jnp.dot(act[...], wout[layer, :, cols], preferred_element_type=F32)
            part[:, :, cols] = total.reshape(steps, SEQS, 256).astype(BF16)

    @pl.loop(0, n_stages + 4)
    def _(i):
        layer, chunk = lax.div(i, n_chunks), lax.rem(i, n_chunks)
        live = i < n_stages

        @pl.when(jnp.logical_and(i >= 1, i <= n_stages))
        def _():
            s = i - 1
            phase0(s).wait()

            @pl.loop(0, half // 4)
            def _(g):
                ts = pl.ds(g * 4, 4)
                sum0[ts] = part[pl.ds(base0 + g * 4, 4)] + recv0[lax.rem(s, 2), ts]

            phase1(s).start()

        @pl.when(live)
        def _():
            norm_and_project(i, layer, chunk)

        @pl.when(jnp.logical_and(i >= 2, i <= n_stages + 1))
        def _():
            s = i - 2
            where = lax.rem(s, n_chunks)
            phase2(s).wait()
            own = pl.ds(base2, eighth)
            total = sum1[pl.ds(eighth * pos2, eighth)].astype(F32) + recv2[lax.rem(s, 2)].astype(F32)
            total = total + hid[where, own].astype(F32) + b_out[lax.div(s, n_chunks)][None]
            hid[where, own] = total.astype(BF16)
            phase3(s).start()

        @pl.when(jnp.logical_and(i >= 3, i <= n_stages + 2))
        def _():
            phase4(i - 3).wait()
            phase5(i - 3).start()

        @pl.when(i >= 4)
        def _():
            s = i - 4
            phase5(s).wait()

            @pl.when(s >= n_stages - n_chunks)
            def _():
                out_copy(lax.rem(s, n_chunks)).start()

        @pl.when(live)
        def _():
            @pl.when(i >= 1)
            def _():
                for copy in rec_copies(i - 1):
                    copy.wait()

            @pl.when(i + 1 < n_stages)
            def _():
                for copy in kv_copies(i + 1):
                    copy.start()

            attend(i, layer, chunk)

        @pl.when(jnp.logical_and(i >= 1, i <= n_stages))
        def _():
            s = i - 1
            phase1(s).wait()

            @pl.loop(0, quarter // 4)
            def _(g):
                ts = pl.ds(g * 4, 4)
                sum1[ts] = sum0[pl.ds(quarter * pos1 + g * 4, 4)] + recv1[lax.rem(s, 2), ts]

            phase2(s).start()

        @pl.when(live)
        def _():
            feed_forward(layer, chunk)

        @pl.when(jnp.logical_and(i >= 2, i <= n_stages + 1))
        def _():
            phase3(i - 2).wait()
            phase4(i - 2).start()

        @pl.when(live)
        def _():
            project_out(i, layer)
            phase0(i).start()

    for copy in rec_copies(n_stages - 1):
        copy.wait()
    for chunk in range(n_chunks):
        out_copy(chunk).wait()


def merge_kernel(n_blocks, lens, k_hbm, v_hbm, rec_k, rec_v, k_out, v_out, kbuf, vbuf, rk, rv, in_sem, out_sem):
    size = kbuf.shape[1]
    steps = rk.shape[2]

    def loads(i):
        slot, here = lax.rem(i, 2), pl.ds(i * size, size)
        return [pltpu.make_async_copy(src.at[here], dst.at[slot], in_sem.at[j, slot])
                for j, (src, dst) in enumerate(((k_hbm, kbuf), (v_hbm, vbuf), (rec_k, rk), (rec_v, rv)))]

    def stores(i):
        slot, here = lax.rem(i, 2), pl.ds(i * size, size)
        return [pltpu.make_async_copy(src.at[slot], dst.at[here], out_sem.at[j, slot])
                for j, (src, dst) in enumerate(((kbuf, k_out), (vbuf, v_out)))]

    for copy in loads(0):
        copy.start()

    @pl.loop(0, n_blocks)
    def _(i):
        slot = lax.rem(i, 2)

        @pl.when(i >= 1)
        def _():
            for copy in stores(i - 1):
                copy.wait()

        @pl.when(i + 1 < n_blocks)
        def _():
            for copy in loads(i + 1):
                copy.start()

        for copy in loads(i):
            copy.wait()
        for b in range(size):
            at = lens[lax.rem(i * size + b, lens.shape[0])]
            kbuf[slot, b, pl.ds(at, steps)] = rk[slot, b]
            vbuf[slot, b, pl.ds(at, steps)] = rv[slot, b]
        for copy in stores(i):
            copy.start()

    for copy in stores(n_blocks - 1):
        copy.wait()


def angle_tables(positions):
    lane = jnp.arange(128)
    inv_freq = jnp.where(lane < ROT_DIM, 1.0 / (10000.0 ** ((lane // 2 * 2).astype(F32) / ROT_DIM)), 0.0)
    angles = positions.astype(F32)[:, None] * inv_freq[None, :]
    return jnp.cos(angles), jnp.where(lane % 2 == 0, -jnp.sin(angles), jnp.sin(angles))


def decode_shard(x_steps, cur_len, k_cache, v_cache, ln_gain, ln_bias, w_q, w_k, w_v, w_o, w_in, b_in, w_out, b_out):
    n_layers, batch, cache_len, n_heads, head_dim = k_cache.shape
    steps, _, d_model = x_steps.shape
    ff = w_in.shape[2]
    n_chunks = batch // SEQS
    n_stages = n_layers * n_chunks
    rows = steps * SEQS
    flat = (n_layers, batch, cache_len * n_heads, head_dim)
    cos_c, sin_c = angle_tables(cur_len)
    cos_t, sin_t = (jnp.broadcast_to(tab[:, None, :], (steps, SEQS, 128)) for tab in angle_tables(jnp.arange(steps)))
    col_slot = jnp.arange(cache_len * n_heads) // n_heads
    old_mask = jnp.where((col_slot[None, :] < cur_len[:, None]) & (col_slot[None, :] < OLD), 1.0, 0.0).astype(F32)
    vecs = [v.astype(F32)[:, None, :] for v in (ln_gain, ln_bias, b_in, b_out)]
    any_spec, vmem = pl.BlockSpec(memory_space=pl.ANY), pl.BlockSpec(memory_space=pltpu.VMEM)
    dma = pltpu.SemaphoreType.DMA
    block = (steps, SEQS, d_model)
    hidden, rec_k, rec_v = pl.pallas_call(
        functools.partial(decode_kernel, n_chunks, n_stages),
        out_shape=(jax.ShapeDtypeStruct(x_steps.shape, BF16),
                   jax.ShapeDtypeStruct((n_layers, batch, steps * n_heads, head_dim), BF16),
                   jax.ShapeDtypeStruct((n_layers, batch, steps * n_heads, head_dim), BF16)),
        in_specs=[any_spec] * 9 + [vmem] * 9,
        out_specs=(any_spec,) * 3,
        scratch_shapes=[
            pltpu.VMEM(w_q.shape, BF16), pltpu.VMEM(w_k.shape, BF16), pltpu.VMEM(w_v.shape, BF16), pltpu.VMEM(w_o.shape, BF16),
            pltpu.VMEM(w_in.shape, BF16), pltpu.VMEM(w_out.shape, BF16),
            pltpu.VMEM((n_chunks,) + block, BF16), pltpu.VMEM(block, BF16),
            pltpu.VMEM((2, steps // 2, SEQS, d_model), BF16), pltpu.VMEM((steps // 2, SEQS, d_model), BF16),
            pltpu.VMEM((2, steps // 4, SEQS, d_model), BF16), pltpu.VMEM((steps // 4, SEQS, d_model), BF16),
            pltpu.VMEM((2, steps // 8, SEQS, d_model), BF16),
            pltpu.VMEM((rows, d_model), BF16),
            pltpu.VMEM((2, rows, 128), F32), pltpu.VMEM((2, rows, 128), F32), pltpu.VMEM((2, rows, 128), F32), pltpu.VMEM((2, rows, 128), F32),
            pltpu.VMEM((rows, 256), BF16), pltpu.VMEM((rows, ff), BF16),
            pltpu.VMEM((SEQS, 2, 2 * steps, 128), F32), pltpu.VMEM((SEQS, 2 * steps, 256), F32),
            pltpu.VMEM((2, SEQS, 256, 128), BF16), pltpu.VMEM((2, SEQS, 256, 128), BF16),
            dma((n_layers, 6)), dma((n_chunks,)), dma((2, 2)), dma((2, 2)), dma((n_chunks,)), dma((6, 2)), dma((6, 4)),
        ],
        compiler_params=pltpu.CompilerParams(collective_id=0, has_side_effects=True, vmem_limit_bytes=60 * 1024 * 1024),
        name="decode",
    )(x_steps, k_cache.reshape(flat), v_cache.reshape(flat), w_q, w_k, w_v, w_o, w_in, w_out,
      cos_c, sin_c, cos_t, sin_t, old_mask, *vecs)

    pairs = n_layers * batch
    size = 16
    lines = (pairs, cache_len, n_heads, head_dim)
    new = (pairs, steps, n_heads, head_dim)
    k_out, v_out = pl.pallas_call(
        functools.partial(merge_kernel, pairs // size),
        out_shape=(jax.ShapeDtypeStruct(lines, BF16),) * 2,
        in_specs=[pl.BlockSpec(memory_space=pltpu.SMEM)] + [any_spec] * 4,
        out_specs=(any_spec,) * 2,
        scratch_shapes=[pltpu.VMEM((2, size) + lines[1:], BF16), pltpu.VMEM((2, size) + lines[1:], BF16),
                        pltpu.VMEM((2, size) + new[1:], BF16), pltpu.VMEM((2, size) + new[1:], BF16), dma((4, 2)), dma((2, 2))],
        name="merge",
    )(cur_len, k_cache.reshape(lines), v_cache.reshape(lines), rec_k.reshape(new), rec_v.reshape(new))
    return hidden, k_out.reshape(k_cache.shape), v_out.reshape(v_cache.shape)


def solution(mesh):
    cache_spec = P(None, "dp", None, "tp", None)
    in_specs = (P(None, "dp", None), P("dp"), cache_spec, cache_spec, P(None, None), P(None, None),
                P(None, None, "tp"), P(None, None, "tp"), P(None, None, "tp"), P(None, "tp", None),
                P(None, None, "tp"), P(None, "tp"), P(None, "tp", None), P(None, None))
    out_specs = (P(None, "dp", None), cache_spec, cache_spec)
    return jax.shard_map(decode_shard, mesh=mesh, in_specs=in_specs, out_specs=out_specs, check_vma=False)
```

time: 5840 us -> 272 us (0.05)
  local copies, waits for them, and re-layouts: 2840 us -> 15 us
  waiting for transfers between devices: 1350 us -> 0 us
  matrix products: 1170 us -> 0 us
  other arithmetic: 397 us -> 3.02 us
  Pallas kernels: 0 us -> 253 us
    psum x33 -> x0, waiting for transfers between devices: 1350 us -> none  [decode_shard(): layer_sum = lax.psum(layer_part.astype(jnp.bfloat16), 'tp')]
    squeeze x128 -> x0, local copies, waits for them, and re-layouts: 1320 us -> none  [the longest x64 666 us: layer_update(): v_cache[layer_idx]]
    dot_general x448 -> x0, matrix products: 1170 us -> none  [the longest x64 381 us: layer_update(): jnp.dot(gelu_act, out_weight, preferred_element_type=jnp.float32)]
    scatter x128 -> x0, local copies, waits for them, and re-layouts: 1140 us -> none  [the longest x64 581 us: layer_update(): k_cache = k_cache.at[layer_idx, batch_rows, new_pos].set(key_new)]
    pallas_call x0 -> x2, Pallas kernels: none -> 253 us  [the longest x1 236 us: decode_shard(): pl.pallas_call(functools.partial(decode_kernel, n_chunks, n_stages), out_...]
    slice x256 -> x0, local copies, waits for them, and re-layouts: 169 us -> none  [the longest x128 94.5 us: apply_rotary(): pairs = vectors[..., :ROT_DIM].reshape(lead_shape + (ROT_DIM // 2, 2))]
    reshape x192 -> x0, local copies, waits for them, and re-layouts: 132 us -> none  [the longest x128 88.7 us: apply_rotary(): rotated.reshape(lead_shape + (ROT_DIM,))]
    another operation x193 -> x0, other arithmetic: 127 us -> none  [the longest x128 67.6 us: apply_rotary(): jnp.stack([even_part * cos_tab - odd_part * sin_tab, odd_part * cos_tab +...]
  transfers between devices with their start and end apart: 33 -> 0, of which waited for: 32 -> 0; matrix products, arithmetic and copies ran while one was open for 16% -> 0% of each run, Pallas kernels for 0% -> 0%
where the time goes in v2:
time: 272 us
  Pallas kernels  253 us (93%)
  local copies, waits for them, and re-layouts  15 us (6%)
  other arithmetic  3.02 us (1%)
    pallas_call x1, Pallas kernels, decode_shard(): pl.pallas_call(functools.partial(decode_kernel, n_chunks, n_stages), out_...  236 us
    pallas_call x1, Pallas kernels, decode_shard(): pl.pallas_call(functools.partial(merge_kernel, pairs // size), out_shape=...  16.5 us
    unnamed x1, local copies, waits for them, and re-layouts  8.44 us

profile of v2, /device:TPU:0, one launch (start us, length us, event | category | flops | bytes accessed | tf_op | source)
XLA Modules:
  0.0 271.5 jit_solution(5003020086594599741)
XLA Ops:
  0.7 0.7 convert_element_type.28
  1.3 1.3 reshape.142.b_in
  2.6 1.3 reshape.140.gain
  3.9 1.3 reshape.141.bias
  5.2 1.3 reshape.143.b_out
  6.5 0.1 negate_select_fusion.1
  6.7 1.4 and_select_fusion.old_mask
  8.1 0.8 negate_select_fusion
  8.9 0.7 broadcast_in_dim.64.sin_t
  9.5 0.7 broadcast_in_dim.62.cos_t
  10.2 236.4 %decode.1 = (bf16[32,64,2048]{2,1,0:T(8,128)(2,1)}, bf16[2,64,64,128]{3,2,1,0:T(8,128)(2,1)}, bf16[2,64,64,128]{3,2,1,0:T(8,128)(2,1)}) custom-call(bf16[32,64,2048]{2,1,0:T(8,128)(2,1)} %x_hbm.1, bf16[2,64,256,128]{3,2,1,0:T(8,128)(2,1)} %bitcast.8, bf16[2,64,256,128]{3,2,1,0:T(8,128)(2,1)} %bitcast.10, bf16[2,2048,256]{2,1,0:T(8,128)(2,1)} %wq_hbm.1, ...), custom_call_target="tpu_custom_call" | custom-call | tf_op jit(solution)/shard_map/decode/pallas_call | solution.py:365
  246.6 16.5 %merge.1 = (bf16[128,128,2,128]{3,2,1,0:T(2,128)(2,1)}, bf16[128,128,2,128]{3,2,1,0:T(2,128)(2,1)}) custom-call(s32[64]{0:T(128)} %lens.1, bf16[128,128,2,128]{3,2,1,0:T(2,128)(2,1)} %bitcast.9, bf16[128,128,2,128]{3,2,1,0:T(2,128)(2,1)} %bitcast.11, bf16[128,32,2,128]{3,2,1,0:T(2,128)(2,1)} %bitcast.12, bf16[128,32,2,128]{3,2,1,0:T(2,128)(2,1)} %bitcast.13), custom_call_target="tpu_custom_call" | custom-call | tf_op jit(solution)/shard_map/merge/pallas_call | solution.py:395
  263.1 8.4 %copy.18 = bf16[32,64,2048]{2,1,0:T(8,128)(2,1)} copy(bf16[32,64,2048]{2,1,0:T(8,128)(2,1)} %get-tuple-element.20) | data formatting | bytes 16777216
  (5 shorter events, 0.0 us)

commit v3 on v2

--- a/solution.py
+++ b/solution.py
@@ -2,6 +2,7 @@
 
 import jax
 import jax.numpy as jnp
+import numpy as np
 from jax import lax
 from jax.experimental import pallas as pl
 from jax.experimental.pallas import tpu as pltpu
@@ -17,10 +18,11 @@
 
 
 def decode_kernel(n_chunks, n_stages, x_hbm, k_hbm, v_hbm, wq_hbm, wk_hbm, wv_hbm, wo_hbm, win_hbm, wout_hbm,
-                  cos_c, sin_c, cos_t, sin_t, old_mask, gain, bias, b_in, b_out,
+                  lens, inv_freq, cos_t, sin_t, gain_in, bias_in, b_in_in, b_out_in,
                   out_hbm, rec_k, rec_v,
                   wq, wk, wv, wo, win, wout, hid, part, recv0, sum0, recv1, sum1, recv2,
                   normed, qf, kf, vf, cf, ctx, act, inter, scores, kbuf, vbuf,
+                  cos_c, sin_c, gain, bias, b_in, b_out,
                   w_sem, x_sem, kv_sem, rec_sem, out_sem, send_sem, recv_sem):
     steps = x_hbm.shape[0]
     rows = steps * SEQS
@@ -75,7 +77,7 @@
         return remote(0, stage, part.at[pl.ds(half - base0, half)], recv0.at[lax.rem(stage, 2)], partner)
 
     def phase1(stage):
-        return remote(1, stage, sum0.at[pl.ds(quarter * (1 - pos1), quarter)], recv1.at[lax.rem(stage, 2)], first)
+        return remote(1, stage, sum0.at[lax.rem(stage, 2), pl.ds(quarter * (1 - pos1), quarter)], recv1.at[lax.rem(stage, 4)], first)
 
     def phase2(stage):
         return remote(2, stage, sum1.at[pl.ds(eighth * (1 - pos2), eighth)], recv2.at[lax.rem(stage, 2)], second)
@@ -107,6 +109,13 @@
         x_copy(chunk).start()
     for j in range(6):
         weight_copy(1, j).start()
+    angles = lens[:, 0:128].astype(F32) * inv_freq[...]
+    odd = lax.rem(lax.broadcasted_iota(jnp.int32, angles.shape, 1), 2) == 1
+    cos_c[...] = jnp.cos(angles)
+    sin_c[...] = jnp.where(odd, jnp.sin(angles), -jnp.sin(angles))
+    for src, dst in ((gain_in, gain), (bias_in, bias), (b_in_in, b_in), (b_out_in, b_out)):
+        for layer in range(src.shape[0]):
+            dst[layer] = src[layer:layer + 1, :].astype(F32)
     pl.semaphore_wait(barrier, 3)
 
     def norm_and_project(stage, layer, chunk):
@@ -154,11 +163,11 @@
         row, col = lax.broadcasted_iota(jnp.int32, shape, 0), lax.broadcasted_iota(jnp.int32, shape, 1)
         col_slot, col_head = lax.shift_right_logical(col, 1), lax.bitwise_and(col, 1)
         row_head, row_step = lax.div(row, steps), lax.rem(row, steps)
-        same = row_head == col_head
-        fresh = jnp.where(col_slot - OLD <= row_step, 2.0, 0.0)
-        kind = jnp.where(same, jnp.where(col_slot >= OLD, fresh, 1.0), 0.0)
+        never = 1 << 20
+        fresh = jnp.where(col_slot - OLD <= row_step, -1, never)
+        key = jnp.where(row_head == col_head, jnp.where(col_slot >= OLD, fresh, col_slot), never)
         here = pl.ds(pl.multiple_of(chunk * SEQS, SEQS), SEQS)
-        old = old_mask[here, :]
+        limit = lens[here, :]
         for b in range(SEQS):
             mine = pl.ds(b, steps, stride=SEQS)
             for src, buf, j in ((kf, kbuf, 0), (vf, vbuf, 1)):
@@ -171,7 +180,7 @@
             mine = pl.ds(b, steps, stride=SEQS)
             query = jnp.concatenate([qf[0, mine, :], qf[1, mine, :]], axis=0).astype(BF16)
             s = lax.dot_general(query, kbuf[slot, b], (((1,), (1,)), ((), ())), preferred_element_type=F32) * (128 ** -0.5)
-            scores[b] = jnp.where(kind + old[b:b + 1, :] > 1.5, s, -jnp.inf)
+            scores[b] = jnp.where(key < limit[b:b + 1, :], s, -jnp.inf)
         for b in range(SEQS):
             s = scores[b]
             e = jnp.exp(s - jnp.max(s, axis=-1, keepdims=True))
@@ -203,12 +212,31 @@
             total += jnp.dot(act[...], wout[layer, :, cols], preferred_element_type=F32)
             part[:, :, cols] = total.reshape(steps, SEQS, 256).astype(BF16)
 
-    @pl.loop(0, n_stages + 4)
+    def between(i, lag):
+        return jnp.logical_and(i >= lag, i < n_stages + lag)
+
+    @pl.loop(0, n_stages + 5)
     def _(i):
         layer, chunk = lax.div(i, n_chunks), lax.rem(i, n_chunks)
         live = i < n_stages
 
-        @pl.when(jnp.logical_and(i >= 1, i <= n_stages))
+        @pl.when(live)
+        def _():
+            norm_and_project(i, layer, chunk)
+
+            @pl.when(i >= 1)
+            def _():
+                for copy in rec_copies(i - 1):
+                    copy.wait()
+
+            @pl.when(i + 1 < n_stages)
+            def _():
+                for copy in kv_copies(i + 1):
+                    copy.start()
+
+            attend(i, layer, chunk)
+
+        @pl.when(between(i, 1))
         def _():
             s = i - 1
             phase0(s).wait()
@@ -216,15 +244,39 @@
             @pl.loop(0, half // 4)
             def _(g):
                 ts = pl.ds(g * 4, 4)
-                sum0[ts] = part[pl.ds(base0 + g * 4, 4)] + recv0[lax.rem(s, 2), ts]
+                sum0[lax.rem(s, 2), ts] = part[pl.ds(base0 + g * 4, 4)] + recv0[lax.rem(s, 2), ts]
 
             phase1(s).start()
 
+        @pl.when(between(i, 3))
+        def _():
+            phase3(i - 3).wait()
+            phase4(i - 3).start()
+
+        @pl.when(between(i, 2))
+        def _():
+            s = i - 2
+            phase1(s).wait()
+
+            @pl.loop(0, quarter // 4)
+            def _(g):
+                ts = pl.ds(g * 4, 4)
+                sum1[ts] = sum0[lax.rem(s, 2), pl.ds(quarter * pos1 + g * 4, 4)] + recv1[lax.rem(s, 4), ts]
+
+            phase2(s).start()
+
+        @pl.when(between(i, 4))
+        def _():
+            phase4(i - 4).wait()
+            phase5(i - 4).start()
+
         @pl.when(live)
         def _():
-            norm_and_project(i, layer, chunk)
-
-        @pl.when(jnp.logical_and(i >= 2, i <= n_stages + 1))
+            feed_forward(layer, chunk)
+            project_out(i, layer)
+            phase0(i).start()
+
+        @pl.when(between(i, 2))
         def _():
             s = i - 2
             where = lax.rem(s, n_chunks)
@@ -235,12 +287,7 @@
             hid[where, own] = total.astype(BF16)
             phase3(s).start()
 
-        @pl.when(jnp.logical_and(i >= 3, i <= n_stages + 2))
-        def _():
-            phase4(i - 3).wait()
-            phase5(i - 3).start()
-
-        @pl.when(i >= 4)
+        @pl.when(between(i, 4))
         def _():
             s = i - 4
             phase5(s).wait()
@@ -248,46 +295,6 @@
             @pl.when(s >= n_stages - n_chunks)
             def _():
                 out_copy(lax.rem(s, n_chunks)).start()
-
-        @pl.when(live)
-        def _():
-            @pl.when(i >= 1)
-            def _():
-                for copy in rec_copies(i - 1):
-                    copy.wait()
-
-            @pl.when(i + 1 < n_stages)
-            def _():
-                for copy in kv_copies(i + 1):
-                    copy.start()
-
-            attend(i, layer, chunk)
-
-        @pl.when(jnp.logical_and(i >= 1, i <= n_stages))
-        def _():
-            s = i - 1
-            phase1(s).wait()
-
-            @pl.loop(0, quarter // 4)
-            def _(g):
-                ts = pl.ds(g * 4, 4)
-                sum1[ts] = sum0[pl.ds(quarter * pos1 + g * 4, 4)] + recv1[lax.rem(s, 2), ts]
-
-            phase2(s).start()
-
-        @pl.when(live)
-        def _():
-            feed_forward(layer, chunk)
-
-        @pl.when(jnp.logical_and(i >= 2, i <= n_stages + 1))
-        def _():
-            phase3(i - 2).wait()
-            phase4(i - 2).start()
-
-        @pl.when(live)
-        def _():
-            project_out(i, layer)
-            phase0(i).start()
 
     for copy in rec_copies(n_stages - 1):
         copy.wait()
@@ -295,35 +302,37 @@
         out_copy(chunk).wait()
 
 
-def merge_kernel(n_blocks, lens, k_hbm, v_hbm, rec_k, rec_v, k_out, v_out, kbuf, vbuf, rk, rv, in_sem, out_sem):
-    size = kbuf.shape[1]
+def merge_kernel(n_blocks, lens, hid_in, k_hbm, v_hbm, rec_k, rec_v, hid_out, k_out, v_out, hbuf, kbuf, vbuf, rk, rv, in_sem, out_sem):
+    depth, size = kbuf.shape[:2]
     steps = rk.shape[2]
+    ahead = depth // 2
 
     def loads(i):
-        slot, here = lax.rem(i, 2), pl.ds(i * size, size)
-        return [pltpu.make_async_copy(src.at[here], dst.at[slot], in_sem.at[j, slot])
-                for j, (src, dst) in enumerate(((k_hbm, kbuf), (v_hbm, vbuf), (rec_k, rk), (rec_v, rv)))]
+        slot = lax.rem(i, depth)
+        pairs = ((hid_in, hbuf), (k_hbm, kbuf), (v_hbm, vbuf), (rec_k, rk), (rec_v, rv))
+        return [pltpu.make_async_copy(src.at[pl.ds(i * dst.shape[1], dst.shape[1])], dst.at[slot], in_sem.at[j, slot]) for j, (src, dst) in enumerate(pairs)]
 
     def stores(i):
-        slot, here = lax.rem(i, 2), pl.ds(i * size, size)
-        return [pltpu.make_async_copy(src.at[slot], dst.at[here], out_sem.at[j, slot])
-                for j, (src, dst) in enumerate(((kbuf, k_out), (vbuf, v_out)))]
-
-    for copy in loads(0):
-        copy.start()
+        slot = lax.rem(i, depth)
+        pairs = ((hbuf, hid_out), (kbuf, k_out), (vbuf, v_out))
+        return [pltpu.make_async_copy(src.at[slot], dst.at[pl.ds(i * src.shape[1], src.shape[1])], out_sem.at[j, slot]) for j, (src, dst) in enumerate(pairs)]
+
+    for i in range(ahead):
+        for copy in loads(i):
+            copy.start()
 
     @pl.loop(0, n_blocks)
     def _(i):
-        slot = lax.rem(i, 2)
-
-        @pl.when(i >= 1)
-        def _():
-            for copy in stores(i - 1):
+        slot = lax.rem(i, depth)
+
+        @pl.when(i >= depth - ahead)
+        def _():
+            for copy in stores(i - (depth - ahead)):
                 copy.wait()
 
-        @pl.when(i + 1 < n_blocks)
-        def _():
-            for copy in loads(i + 1):
+        @pl.when(i + ahead < n_blocks)
+        def _():
+            for copy in loads(i + ahead):
                 copy.start()
 
         for copy in loads(i):
@@ -335,15 +344,14 @@
         for copy in stores(i):
             copy.start()
 
-    for copy in stores(n_blocks - 1):
-        copy.wait()
-
-
-def angle_tables(positions):
-    lane = jnp.arange(128)
-    inv_freq = jnp.where(lane < ROT_DIM, 1.0 / (10000.0 ** ((lane // 2 * 2).astype(F32) / ROT_DIM)), 0.0)
-    angles = positions.astype(F32)[:, None] * inv_freq[None, :]
-    return jnp.cos(angles), jnp.where(lane % 2 == 0, -jnp.sin(angles), jnp.sin(angles))
+    for i in range(n_blocks - (depth - ahead), n_blocks):
+        for copy in stores(i):
+            copy.wait()
+
+
+def inverse_frequencies():
+    lane = np.arange(128)
+    return np.where(lane < ROT_DIM, 1.0 / (10000.0 ** ((lane // 2 * 2) / ROT_DIM)), 0.0)
 
 
 def decode_shard(x_steps, cur_len, k_cache, v_cache, ln_gain, ln_bias, w_q, w_k, w_v, w_o, w_in, b_in, w_out, b_out):
@@ -354,11 +362,11 @@
     n_stages = n_layers * n_chunks
     rows = steps * SEQS
     flat = (n_layers, batch, cache_len * n_heads, head_dim)
-    cos_c, sin_c = angle_tables(cur_len)
-    cos_t, sin_t = (jnp.broadcast_to(tab[:, None, :], (steps, SEQS, 128)) for tab in angle_tables(jnp.arange(steps)))
-    col_slot = jnp.arange(cache_len * n_heads) // n_heads
-    old_mask = jnp.where((col_slot[None, :] < cur_len[:, None]) & (col_slot[None, :] < OLD), 1.0, 0.0).astype(F32)
-    vecs = [v.astype(F32)[:, None, :] for v in (ln_gain, ln_bias, b_in, b_out)]
+    step_angles = np.arange(steps)[:, None] * inverse_frequencies()[None, :]
+    signed = np.where(np.arange(128) % 2 == 0, -1.0, 1.0)
+    cos_t, sin_t = (np.repeat(tab.astype(np.float32)[:, None, :], SEQS, axis=1) for tab in (np.cos(step_angles), np.sin(step_angles) * signed))
+    inv_freq = np.broadcast_to(inverse_frequencies().astype(np.float32), (batch, 128))
+    lens = jnp.broadcast_to(cur_len[:, None], (batch, cache_len * n_heads))
     any_spec, vmem = pl.BlockSpec(memory_space=pl.ANY), pl.BlockSpec(memory_space=pltpu.VMEM)
     dma = pltpu.SemaphoreType.DMA
     block = (steps, SEQS, d_model)
@@ -367,40 +375,45 @@
         out_shape=(jax.ShapeDtypeStruct(x_steps.shape, BF16),
                    jax.ShapeDtypeStruct((n_layers, batch, steps * n_heads, head_dim), BF16),
                    jax.ShapeDtypeStruct((n_layers, batch, steps * n_heads, head_dim), BF16)),
-        in_specs=[any_spec] * 9 + [vmem] * 9,
+        in_specs=[any_spec] * 9 + [vmem] * 8,
         out_specs=(any_spec,) * 3,
         scratch_shapes=[
             pltpu.VMEM(w_q.shape, BF16), pltpu.VMEM(w_k.shape, BF16), pltpu.VMEM(w_v.shape, BF16), pltpu.VMEM(w_o.shape, BF16),
             pltpu.VMEM(w_in.shape, BF16), pltpu.VMEM(w_out.shape, BF16),
             pltpu.VMEM((n_chunks,) + block, BF16), pltpu.VMEM(block, BF16),
-            pltpu.VMEM((2, steps // 2, SEQS, d_model), BF16), pltpu.VMEM((steps // 2, SEQS, d_model), BF16),
-            pltpu.VMEM((2, steps // 4, SEQS, d_model), BF16), pltpu.VMEM((steps // 4, SEQS, d_model), BF16),
+            pltpu.VMEM((2, steps // 2, SEQS, d_model), BF16), pltpu.VMEM((2, steps // 2, SEQS, d_model), BF16),
+            pltpu.VMEM((4, steps // 4, SEQS, d_model), BF16), pltpu.VMEM((steps // 4, SEQS, d_model), BF16),
             pltpu.VMEM((2, steps // 8, SEQS, d_model), BF16),
             pltpu.VMEM((rows, d_model), BF16),
             pltpu.VMEM((2, rows, 128), F32), pltpu.VMEM((2, rows, 128), F32), pltpu.VMEM((2, rows, 128), F32), pltpu.VMEM((2, rows, 128), F32),
             pltpu.VMEM((rows, 256), BF16), pltpu.VMEM((rows, ff), BF16),
             pltpu.VMEM((SEQS, 2, 2 * steps, 128), F32), pltpu.VMEM((SEQS, 2 * steps, 256), F32),
             pltpu.VMEM((2, SEQS, 256, 128), BF16), pltpu.VMEM((2, SEQS, 256, 128), BF16),
+            pltpu.VMEM((batch, 128), F32), pltpu.VMEM((batch, 128), F32),
+            pltpu.VMEM((n_layers, 1, d_model), F32), pltpu.VMEM((n_layers, 1, d_model), F32),
+            pltpu.VMEM((n_layers, 1, ff), F32), pltpu.VMEM((n_layers, 1, d_model), F32),
             dma((n_layers, 6)), dma((n_chunks,)), dma((2, 2)), dma((2, 2)), dma((n_chunks,)), dma((6, 2)), dma((6, 4)),
         ],
         compiler_params=pltpu.CompilerParams(collective_id=0, has_side_effects=True, vmem_limit_bytes=60 * 1024 * 1024),
         name="decode",
     )(x_steps, k_cache.reshape(flat), v_cache.reshape(flat), w_q, w_k, w_v, w_o, w_in, w_out,
-      cos_c, sin_c, cos_t, sin_t, old_mask, *vecs)
+      lens, inv_freq, cos_t, sin_t, ln_gain, ln_bias, b_in, b_out)
 
     pairs = n_layers * batch
-    size = 16
+    n_blocks, depth = 16, 4
+    size = pairs // n_blocks
     lines = (pairs, cache_len, n_heads, head_dim)
     new = (pairs, steps, n_heads, head_dim)
-    k_out, v_out = pl.pallas_call(
-        functools.partial(merge_kernel, pairs // size),
-        out_shape=(jax.ShapeDtypeStruct(lines, BF16),) * 2,
-        in_specs=[pl.BlockSpec(memory_space=pltpu.SMEM)] + [any_spec] * 4,
-        out_specs=(any_spec,) * 2,
-        scratch_shapes=[pltpu.VMEM((2, size) + lines[1:], BF16), pltpu.VMEM((2, size) + lines[1:], BF16),
-                        pltpu.VMEM((2, size) + new[1:], BF16), pltpu.VMEM((2, size) + new[1:], BF16), dma((4, 2)), dma((2, 2))],
+    hidden, k_out, v_out = pl.pallas_call(
+        functools.partial(merge_kernel, n_blocks),
+        out_shape=(jax.ShapeDtypeStruct(x_steps.shape, BF16),) + (jax.ShapeDtypeStruct(lines, BF16),) * 2,
+        in_specs=[pl.BlockSpec(memory_space=pltpu.SMEM)] + [any_spec] * 5,
+        out_specs=(any_spec,) * 3,
+        scratch_shapes=[pltpu.VMEM((depth, steps // n_blocks) + x_steps.shape[1:], BF16),
+                        pltpu.VMEM((depth, size) + lines[1:], BF16), pltpu.VMEM((depth, size) + lines[1:], BF16),
+                        pltpu.VMEM((depth, size) + new[1:], BF16), pltpu.VMEM((depth, size) + new[1:], BF16), dma((5, depth)), dma((3, depth))],
         name="merge",
-    )(cur_len, k_cache.reshape(lines), v_cache.reshape(lines), rec_k.reshape(new), rec_v.reshape(new))
+    )(cur_len, hidden, k_cache.reshape(lines), v_cache.reshape(lines), rec_k.reshape(new), rec_v.reshape(new))
     return hidden, k_out.reshape(k_cache.shape), v_out.reshape(v_cache.shape)
 
 

time: 272 us -> 230 us (0.85)
  Pallas kernels: 253 us -> 227 us
  local copies, waits for them, and re-layouts: 15 us -> 2.63 us
  other arithmetic: 3.02 us -> 0 us
    pallas_call x1, Pallas kernels: 236 us -> 207 us  [decode_shard(): pl.pallas_call(functools.partial(decode_kernel, n_chunks, n_stages), out_...]
    unnamed x1 -> x0, local copies, waits for them, and re-layouts: 8.44 us -> none
    broadcast_in_dim x6 -> x1, local copies, waits for them, and re-layouts: 6.53 us -> 1.36 us  [decode_shard(): lens = jnp.broadcast_to(cur_len[:, None], (batch, cache_len * n_heads))]
    pallas_call x1, Pallas kernels: 16.5 us -> 19.8 us  [decode_shard(): pl.pallas_call(functools.partial(merge_kernel, n_blocks), out_shape=(jax....]
where the time goes in v3:
time: 230 us
  Pallas kernels  227 us (99%)
  local copies, waits for them, and re-layouts  2.63 us (1%)
    pallas_call x1, Pallas kernels, decode_shard(): pl.pallas_call(functools.partial(decode_kernel, n_chunks, n_stages), out_...  207 us
    pallas_call x1, Pallas kernels, decode_shard(): pl.pallas_call(functools.partial(merge_kernel, n_blocks), out_shape=(jax....  19.8 us

profile of v3, /device:TPU:0, one launch (start us, length us, event | category | flops | bytes accessed | tf_op | source)
XLA Modules:
  0.0 230.0 jit_solution(9021638432421353889)
XLA Ops:
  0.6 1.4 broadcast_in_dim.2.lens
  2.0 1.3 jit_solution_.3.inv_freq
  3.3 206.9 %decode.1 = (bf16[32,64,2048]{2,1,0:T(8,128)(2,1)}, bf16[2,64,64,128]{3,2,1,0:T(8,128)(2,1)}, bf16[2,64,64,128]{3,2,1,0:T(8,128)(2,1)}) custom-call(bf16[32,64,2048]{2,1,0:T(8,128)(2,1)} %x_hbm.1, bf16[2,64,256,128]{3,2,1,0:T(8,128)(2,1)} %bitcast.8, bf16[2,64,256,128]{3,2,1,0:T(8,128)(2,1)} %bitcast.10, bf16[2,2048,256]{2,1,0:T(8,128)(2,1)} %wq_hbm.1, ...), custom_call_target="tpu_custom_call" | custom-call | tf_op jit(solution)/shard_map/decode/pallas_call | solution.py:373
  210.2 19.8 %merge.1 = (bf16[32,64,2048]{2,1,0:T(8,128)(2,1)}, bf16[128,128,2,128]{3,2,1,0:T(2,128)(2,1)}, bf16[128,128,2,128]{3,2,1,0:T(2,128)(2,1)}) custom-call(s32[64]{0:T(128)} %lens.1, bf16[32,64,2048]{2,1,0:T(8,128)(2,1)} %get-tuple-element.9.hid_in, bf16[128,128,2,128]{3,2,1,0:T(2,128)(2,1)} %bitcast.9, bf16[128,128,2,128]{3,2,1,0:T(2,128)(2,1)} %bitcast.11, ...), custom_call_target="tpu_custom_call" | custom-call | tf_op jit(solution)/shard_map/merge/pallas_call | solution.py:407

commit v4 on v3

--- a/solution.py
+++ b/solution.py
@@ -80,7 +80,7 @@
         return remote(1, stage, sum0.at[lax.rem(stage, 2), pl.ds(quarter * (1 - pos1), quarter)], recv1.at[lax.rem(stage, 4)], first)
 
     def phase2(stage):
-        return remote(2, stage, sum1.at[pl.ds(eighth * (1 - pos2), eighth)], recv2.at[lax.rem(stage, 2)], second)
+        return remote(2, stage, sum1.at[lax.rem(stage, 2), pl.ds(eighth * (1 - pos2), eighth)], recv2.at[lax.rem(stage, 4)], second)
 
     def gather(phase, stage, start, size, peer):
         block = hid.at[lax.rem(stage, n_chunks), pl.ds(start, size)]
@@ -215,7 +215,7 @@
     def between(i, lag):
         return jnp.logical_and(i >= lag, i < n_stages + lag)
 
-    @pl.loop(0, n_stages + 5)
+    @pl.loop(0, n_stages + 6)
     def _(i):
         layer, chunk = lax.div(i, n_chunks), lax.rem(i, n_chunks)
         live = i < n_stages
@@ -248,11 +248,6 @@
 
             phase1(s).start()
 
-        @pl.when(between(i, 3))
-        def _():
-            phase3(i - 3).wait()
-            phase4(i - 3).start()
-
         @pl.when(between(i, 2))
         def _():
             s = i - 2
@@ -261,14 +256,30 @@
             @pl.loop(0, quarter // 4)
             def _(g):
                 ts = pl.ds(g * 4, 4)
-                sum1[ts] = sum0[lax.rem(s, 2), pl.ds(quarter * pos1 + g * 4, 4)] + recv1[lax.rem(s, 4), ts]
+                sum1[lax.rem(s, 2), ts] = sum0[lax.rem(s, 2), pl.ds(quarter * pos1 + g * 4, 4)] + recv1[lax.rem(s, 4), ts]
 
             phase2(s).start()
 
+        @pl.when(between(i, 3))
+        def _():
+            s = i - 3
+            where = lax.rem(s, n_chunks)
+            phase2(s).wait()
+            own = pl.ds(base2, eighth)
+            total = sum1[lax.rem(s, 2), pl.ds(eighth * pos2, eighth)].astype(F32) + recv2[lax.rem(s, 4)].astype(F32)
+            total = total + hid[where, own].astype(F32) + b_out[lax.div(s, n_chunks)][None]
+            hid[where, own] = total.astype(BF16)
+            phase3(s).start()
+
         @pl.when(between(i, 4))
         def _():
-            phase4(i - 4).wait()
-            phase5(i - 4).start()
+            phase3(i - 4).wait()
+            phase4(i - 4).start()
+
+        @pl.when(between(i, 5))
+        def _():
+            phase4(i - 5).wait()
+            phase5(i - 5).start()
 
         @pl.when(live)
         def _():
@@ -276,20 +287,9 @@
             project_out(i, layer)
             phase0(i).start()
 
-        @pl.when(between(i, 2))
-        def _():
-            s = i - 2
-            where = lax.rem(s, n_chunks)
-            phase2(s).wait()
-            own = pl.ds(base2, eighth)
-            total = sum1[pl.ds(eighth * pos2, eighth)].astype(F32) + recv2[lax.rem(s, 2)].astype(F32)
-            total = total + hid[where, own].astype(F32) + b_out[lax.div(s, n_chunks)][None]
-            hid[where, own] = total.astype(BF16)
-            phase3(s).start()
-
-        @pl.when(between(i, 4))
-        def _():
-            s = i - 4
+        @pl.when(between(i, 5))
+        def _():
+            s = i - 5
             phase5(s).wait()
 
             @pl.when(s >= n_stages - n_chunks)
@@ -382,8 +382,8 @@
             pltpu.VMEM(w_in.shape, BF16), pltpu.VMEM(w_out.shape, BF16),
             pltpu.VMEM((n_chunks,) + block, BF16), pltpu.VMEM(block, BF16),
             pltpu.VMEM((2, steps // 2, SEQS, d_model), BF16), pltpu.VMEM((2, steps // 2, SEQS, d_model), BF16),
-            pltpu.VMEM((4, steps // 4, SEQS, d_model), BF16), pltpu.VMEM((steps // 4, SEQS, d_model), BF16),
-            pltpu.VMEM((2, steps // 8, SEQS, d_model), BF16),
+            pltpu.VMEM((4, steps // 4, SEQS, d_model), BF16), pltpu.VMEM((2, steps // 4, SEQS, d_model), BF16),
+            pltpu.VMEM((4, steps // 8, SEQS, d_model), BF16),
             pltpu.VMEM((rows, d_model), BF16),
             pltpu.VMEM((2, rows, 128), F32), pltpu.VMEM((2, rows, 128), F32), pltpu.VMEM((2, rows, 128), F32), pltpu.VMEM((2, rows, 128), F32),
             pltpu.VMEM((rows, 256), BF16), pltpu.VMEM((rows, ff), BF16),

time: 230 us -> 207 us (0.900)
  Pallas kernels: 227 us -> 204 us
    pallas_call x1, Pallas kernels: 207 us -> 184 us  [decode_shard(): pl.pallas_call(functools.partial(decode_kernel, n_chunks, n_stages), out_...]
where the time goes in v4:
time: 207 us
  Pallas kernels  204 us (99%)
  local copies, waits for them, and re-layouts  2.63 us (1%)
    pallas_call x1, Pallas kernels, decode_shard(): pl.pallas_call(functools.partial(decode_kernel, n_chunks, n_stages), out_...  184 us
    pallas_call x1, Pallas kernels, decode_shard(): pl.pallas_call(functools.partial(merge_kernel, n_blocks), out_shape=(jax....  19.8 us

profile of v4, /device:TPU:0, one launch (start us, length us, event | category | flops | bytes accessed | tf_op | source)
XLA Modules:
  0.0 207.3 jit_solution(5547987075498220499)
XLA Ops:
  0.6 1.4 broadcast_in_dim.2.lens
  2.0 1.3 jit_solution_.3.inv_freq
  3.3 184.2 %decode.1 = (bf16[32,64,2048]{2,1,0:T(8,128)(2,1)}, bf16[2,64,64,128]{3,2,1,0:T(8,128)(2,1)}, bf16[2,64,64,128]{3,2,1,0:T(8,128)(2,1)}) custom-call(bf16[32,64,2048]{2,1,0:T(8,128)(2,1)} %x_hbm.1, bf16[2,64,256,128]{3,2,1,0:T(8,128)(2,1)} %bitcast.8, bf16[2,64,256,128]{3,2,1,0:T(8,128)(2,1)} %bitcast.10, bf16[2,2048,256]{2,1,0:T(8,128)(2,1)} %wq_hbm.1, ...), custom_call_target="tpu_custom_call" | custom-call | tf_op jit(solution)/shard_map/decode/pallas_call | solution.py:373
  187.4 19.8 %merge.1 = (bf16[32,64,2048]{2,1,0:T(8,128)(2,1)}, bf16[128,128,2,128]{3,2,1,0:T(2,128)(2,1)}, bf16[128,128,2,128]{3,2,1,0:T(2,128)(2,1)}) custom-call(s32[64]{0:T(128)} %lens.1, bf16[32,64,2048]{2,1,0:T(8,128)(2,1)} %get-tuple-element.9.hid_in, bf16[128,128,2,128]{3,2,1,0:T(2,128)(2,1)} %bitcast.9, bf16[128,128,2,128]{3,2,1,0:T(2,128)(2,1)} %bitcast.11, ...), custom_call_target="tpu_custom_call" | custom-call | tf_op jit(solution)/shard_map/merge/pallas_call | solution.py:407

commit v5 on v4

--- a/solution.py
+++ b/solution.py
@@ -18,11 +18,11 @@
 
 
 def decode_kernel(n_chunks, n_stages, x_hbm, k_hbm, v_hbm, wq_hbm, wk_hbm, wv_hbm, wo_hbm, win_hbm, wout_hbm,
-                  lens, inv_freq, cos_t, sin_t, gain_in, bias_in, b_in_in, b_out_in,
+                  lens_in, inv_freq, cos_t, sin_t, gain_in, bias_in, b_in_in, b_out_in,
                   out_hbm, rec_k, rec_v,
                   wq, wk, wv, wo, win, wout, hid, part, recv0, sum0, recv1, sum1, recv2,
                   normed, qf, kf, vf, cf, ctx, act, inter, scores, kbuf, vbuf,
-                  cos_c, sin_c, gain, bias, b_in, b_out,
+                  lens, cos_c, sin_c, gain, bias, b_in, b_out,
                   w_sem, x_sem, kv_sem, rec_sem, out_sem, send_sem, recv_sem):
     steps = x_hbm.shape[0]
     rows = steps * SEQS
@@ -109,6 +109,8 @@
         x_copy(chunk).start()
     for j in range(6):
         weight_copy(1, j).start()
+    for b in range(lens.shape[0]):
+        lens[b:b + 1, :] = jnp.full((1, lens.shape[1]), lens_in[b], jnp.int32)
     angles = lens[:, 0:128].astype(F32) * inv_freq[...]
     odd = lax.rem(lax.broadcasted_iota(jnp.int32, angles.shape, 1), 2) == 1
     cos_c[...] = jnp.cos(angles)
@@ -195,7 +197,7 @@
             for j in range(3, 6):
                 weight_copy(layer, j).wait()
 
-        @pl.loop(0, act.shape[1] // 256)
+        @pl.loop(0, act.shape[1] // 256, unroll=2)
         def _(n):
             cols = pl.ds(pl.multiple_of(n * 256, 256), 256)
             pre = jnp.dot(normed[...], win[layer, :, cols], preferred_element_type=F32) + b_in[layer, :, cols]
@@ -205,7 +207,7 @@
         for h in range(2):
             ctx[:, h * 128:(h + 1) * 128] = cf[h].astype(BF16)
 
-        @pl.loop(0, d_model // 256)
+        @pl.loop(0, d_model // 256, unroll=2)
         def _(n):
             cols = pl.ds(pl.multiple_of(n * 256, 256), 256)
             total = jnp.dot(ctx[...], wo[layer, :, cols], preferred_element_type=F32)
@@ -303,48 +305,38 @@
 
 
 def merge_kernel(n_blocks, lens, hid_in, k_hbm, v_hbm, rec_k, rec_v, hid_out, k_out, v_out, hbuf, kbuf, vbuf, rk, rv, in_sem, out_sem):
-    depth, size = kbuf.shape[:2]
-    steps = rk.shape[2]
-    ahead = depth // 2
+    size = kbuf.shape[0] // n_blocks
+    steps = rk.shape[1]
+
+    def block(ref, i):
+        rows = ref.shape[0] // n_blocks
+        return ref.at[pl.ds(i * rows, rows)]
 
     def loads(i):
-        slot = lax.rem(i, depth)
-        pairs = ((hid_in, hbuf), (k_hbm, kbuf), (v_hbm, vbuf), (rec_k, rk), (rec_v, rv))
-        return [pltpu.make_async_copy(src.at[pl.ds(i * dst.shape[1], dst.shape[1])], dst.at[slot], in_sem.at[j, slot]) for j, (src, dst) in enumerate(pairs)]
+        pairs = ((k_hbm, kbuf), (v_hbm, vbuf), (rec_k, rk), (rec_v, rv), (hid_in, hbuf))
+        return [pltpu.make_async_copy(block(src, i), block(dst, i), in_sem.at[j, i]) for j, (src, dst) in enumerate(pairs)]
 
     def stores(i):
-        slot = lax.rem(i, depth)
-        pairs = ((hbuf, hid_out), (kbuf, k_out), (vbuf, v_out))
-        return [pltpu.make_async_copy(src.at[slot], dst.at[pl.ds(i * src.shape[1], src.shape[1])], out_sem.at[j, slot]) for j, (src, dst) in enumerate(pairs)]
-
-    for i in range(ahead):
+        pairs = ((kbuf, k_out), (vbuf, v_out), (hbuf, hid_out))
+        return [pltpu.make_async_copy(block(src, i), block(dst, i), out_sem.at[j, i]) for j, (src, dst) in enumerate(pairs)]
+
+    for i in range(n_blocks):
         for copy in loads(i):
             copy.start()
 
     @pl.loop(0, n_blocks)
     def _(i):
-        slot = lax.rem(i, depth)
-
-        @pl.when(i >= depth - ahead)
-        def _():
-            for copy in stores(i - (depth - ahead)):
-                copy.wait()
-
-        @pl.when(i + ahead < n_blocks)
-        def _():
-            for copy in loads(i + ahead):
-                copy.start()
-
         for copy in loads(i):
             copy.wait()
         for b in range(size):
-            at = lens[lax.rem(i * size + b, lens.shape[0])]
-            kbuf[slot, b, pl.ds(at, steps)] = rk[slot, b]
-            vbuf[slot, b, pl.ds(at, steps)] = rv[slot, b]
+            row = i * size + b
+            at = lens[lax.rem(row, lens.shape[0])]
+            kbuf[row, pl.ds(at, steps)] = rk[row]
+            vbuf[row, pl.ds(at, steps)] = rv[row]
         for copy in stores(i):
             copy.start()
 
-    for i in range(n_blocks - (depth - ahead), n_blocks):
+    for i in range(n_blocks):
         for copy in stores(i):
             copy.wait()
 
@@ -365,8 +357,7 @@
     step_angles = np.arange(steps)[:, None] * inverse_frequencies()[None, :]
     signed = np.where(np.arange(128) % 2 == 0, -1.0, 1.0)
     cos_t, sin_t = (np.repeat(tab.astype(np.float32)[:, None, :], SEQS, axis=1) for tab in (np.cos(step_angles), np.sin(step_angles) * signed))
-    inv_freq = np.broadcast_to(inverse_frequencies().astype(np.float32), (batch, 128))
-    lens = jnp.broadcast_to(cur_len[:, None], (batch, cache_len * n_heads))
+    inv_freq = inverse_frequencies().astype(np.float32)[None, :]
     any_spec, vmem = pl.BlockSpec(memory_space=pl.ANY), pl.BlockSpec(memory_space=pltpu.VMEM)
     dma = pltpu.SemaphoreType.DMA
     block = (steps, SEQS, d_model)
@@ -375,7 +366,7 @@
         out_shape=(jax.ShapeDtypeStruct(x_steps.shape, BF16),
                    jax.ShapeDtypeStruct((n_layers, batch, steps * n_heads, head_dim), BF16),
                    jax.ShapeDtypeStruct((n_layers, batch, steps * n_heads, head_dim), BF16)),
-        in_specs=[any_spec] * 9 + [vmem] * 8,
+        in_specs=[any_spec] * 9 + [pl.BlockSpec(memory_space=pltpu.SMEM)] + [vmem] * 7,
         out_specs=(any_spec,) * 3,
         scratch_shapes=[
             pltpu.VMEM(w_q.shape, BF16), pltpu.VMEM(w_k.shape, BF16), pltpu.VMEM(w_v.shape, BF16), pltpu.VMEM(w_o.shape, BF16),
@@ -389,7 +380,7 @@
             pltpu.VMEM((rows, 256), BF16), pltpu.VMEM((rows, ff), BF16),
             pltpu.VMEM((SEQS, 2, 2 * steps, 128), F32), pltpu.VMEM((SEQS, 2 * steps, 256), F32),
             pltpu.VMEM((2, SEQS, 256, 128), BF16), pltpu.VMEM((2, SEQS, 256, 128), BF16),
-            pltpu.VMEM((batch, 128), F32), pltpu.VMEM((batch, 128), F32),
+            pltpu.VMEM((batch, cache_len * n_heads), jnp.int32), pltpu.VMEM((batch, 128), F32), pltpu.VMEM((batch, 128), F32),
             pltpu.VMEM((n_layers, 1, d_model), F32), pltpu.VMEM((n_layers, 1, d_model), F32),
             pltpu.VMEM((n_layers, 1, ff), F32), pltpu.VMEM((n_layers, 1, d_model), F32),
             dma((n_layers, 6)), dma((n_chunks,)), dma((2, 2)), dma((2, 2)), dma((n_chunks,)), dma((6, 2)), dma((6, 4)),
@@ -397,11 +388,10 @@
         compiler_params=pltpu.CompilerParams(collective_id=0, has_side_effects=True, vmem_limit_bytes=60 * 1024 * 1024),
         name="decode",
     )(x_steps, k_cache.reshape(flat), v_cache.reshape(flat), w_q, w_k, w_v, w_o, w_in, w_out,
-      lens, inv_freq, cos_t, sin_t, ln_gain, ln_bias, b_in, b_out)
+      cur_len, inv_freq, cos_t, sin_t, ln_gain, ln_bias, b_in, b_out)
 
     pairs = n_layers * batch
-    n_blocks, depth = 16, 4
-    size = pairs // n_blocks
+    n_blocks = 16
     lines = (pairs, cache_len, n_heads, head_dim)
     new = (pairs, steps, n_heads, head_dim)
     hidden, k_out, v_out = pl.pallas_call(
@@ -409,9 +399,9 @@
         out_shape=(jax.ShapeDtypeStruct(x_steps.shape, BF16),) + (jax.ShapeDtypeStruct(lines, BF16),) * 2,
         in_specs=[pl.BlockSpec(memory_space=pltpu.SMEM)] + [any_spec] * 5,
         out_specs=(any_spec,) * 3,
-        scratch_shapes=[pltpu.VMEM((depth, steps // n_blocks) + x_steps.shape[1:], BF16),
-                        pltpu.VMEM((depth, size) + lines[1:], BF16), pltpu.VMEM((depth, size) + lines[1:], BF16),
-                        pltpu.VMEM((depth, size) + new[1:], BF16), pltpu.VMEM((depth, size) + new[1:], BF16), dma((5, depth)), dma((3, depth))],
+        scratch_shapes=[pltpu.VMEM(x_steps.shape, BF16), pltpu.VMEM(lines, BF16), pltpu.VMEM(lines, BF16),
+                        pltpu.VMEM(new, BF16), pltpu.VMEM(new, BF16), dma((5, n_blocks)), dma((3, n_blocks))],
+        compiler_params=pltpu.CompilerParams(vmem_limit_bytes=62 * 1024 * 1024),
         name="merge",
     )(cur_len, hidden, k_cache.reshape(lines), v_cache.reshape(lines), rec_k.reshape(new), rec_v.reshape(new))
     return hidden, k_out.reshape(k_cache.shape), v_out.reshape(v_cache.shape)

time: 207 us -> 198 us (0.957)
  Pallas kernels: 204 us -> 197 us
  local copies, waits for them, and re-layouts: 2.63 us -> 0 us
    pallas_call x1, Pallas kernels: 184 us -> 177 us  [decode_shard(): pl.pallas_call(functools.partial(decode_kernel, n_chunks, n_stages), out_...]
where the time goes in v5:
time: 198 us
  Pallas kernels  197 us (99%)
    pallas_call x1, Pallas kernels, decode_shard(): pl.pallas_call(functools.partial(decode_kernel, n_chunks, n_stages), out_...  177 us
    pallas_call x1, Pallas kernels, decode_shard(): pl.pallas_call(functools.partial(merge_kernel, n_blocks), out_shape=(jax....  20.4 us

profile of v5, /device:TPU:0, one launch (start us, length us, event | category | flops | bytes accessed | tf_op | source)
XLA Modules:
  0.0 197.9 jit_solution(473297225987594835)
XLA Ops:
  0.6 176.8 %decode.1 = (bf16[32,64,2048]{2,1,0:T(8,128)(2,1)}, bf16[2,64,64,128]{3,2,1,0:T(8,128)(2,1)}, bf16[2,64,64,128]{3,2,1,0:T(8,128)(2,1)}) custom-call(bf16[32,64,2048]{2,1,0:T(8,128)(2,1)} %x_hbm.1, bf16[2,64,256,128]{3,2,1,0:T(8,128)(2,1)} %bitcast.8, bf16[2,64,256,128]{3,2,1,0:T(8,128)(2,1)} %bitcast.10, bf16[2,2048,256]{2,1,0:T(8,128)(2,1)} %wq_hbm.1, ...), custom_call_target="tpu_custom_call" | custom-call | tf_op jit(solution)/shard_map/decode/pallas_call | solution.py:364
  177.4 20.4 %merge.1 = (bf16[32,64,2048]{2,1,0:T(8,128)(2,1)}, bf16[128,128,2,128]{3,2,1,0:T(2,128)(2,1)}, bf16[128,128,2,128]{3,2,1,0:T(2,128)(2,1)}) custom-call(s32[64]{0:T(128)} %lens.1, bf16[32,64,2048]{2,1,0:T(8,128)(2,1)} %get-tuple-element.9.hid_in, bf16[128,128,2,128]{3,2,1,0:T(2,128)(2,1)} %bitcast.9, bf16[128,128,2,128]{3,2,1,0:T(2,128)(2,1)} %bitcast.11, ...), custom_call_target="tpu_custom_call" | custom-call | tf_op jit(solution)/shard_map/merge/pallas_call | solution.py:397

commit v6 on v5

--- a/solution.py
+++ b/solution.py
@@ -26,7 +26,7 @@
                   w_sem, x_sem, kv_sem, rec_sem, out_sem, send_sem, recv_sem):
     steps = x_hbm.shape[0]
     rows = steps * SEQS
-    half, quarter, eighth = steps // 2, steps // 4, steps // 8
+    half, quarter, eighth, last = steps // 2, steps // 4, steps // 8, steps // 16
     d_model = x_hbm.shape[2]
     me = lax.axis_index("tp")
     core = lax.rem(me, 2)
@@ -35,13 +35,11 @@
     partner = me + 1 - 2 * core
     x_peer = me + 2 * (1 - 2 * px)
     y_peer = me + 4 * (1 - 2 * py)
-    first = (1 - core) * x_peer + core * y_peer
-    second = (1 - core) * y_peer + core * x_peer
-    pos1 = (1 - core) * px + core * py
-    pos2 = (1 - core) * py + core * px
-    base0 = half * core
-    base1 = base0 + quarter * pos1
-    base2 = base1 + eighth * pos2
+    first, second = (x_peer, y_peer), (y_peer, x_peer)
+    pos1, pos2 = (px, py), (py, px)
+    base = half * core
+    base1 = [base + quarter * j + eighth * pos1[j] for j in range(2)]
+    base2 = [base1[j] + last * pos2[j] for j in range(2)]
 
     weight_pairs = ((wq_hbm, wq), (wk_hbm, wk), (wv_hbm, wv), (win_hbm, win), (wo_hbm, wo), (wout_hbm, wout))
 
@@ -68,32 +66,33 @@
         return (pltpu.make_async_copy(kbuf.at[slot, :, new, :], rec_k.at[layer, seqs], rec_sem.at[0, slot]),
                 pltpu.make_async_copy(vbuf.at[slot, :, new, :], rec_v.at[layer, seqs], rec_sem.at[1, slot]))
 
-    def remote(phase, stage, src, dst, peer):
-        slot = lax.rem(stage, 2)
-        return pltpu.make_async_remote_copy(src_ref=src, dst_ref=dst, send_sem=send_sem.at[phase, slot], recv_sem=recv_sem.at[phase, lax.rem(stage, 4)],
-                                            device_id={"tp": peer}, device_id_type=MESH)
+    def remote(kind, stage, src, dst, peer):
+        return pltpu.make_async_remote_copy(src_ref=src, dst_ref=dst, send_sem=send_sem.at[kind, lax.rem(stage, 2)],
+                                            recv_sem=recv_sem.at[kind, lax.rem(stage, 4)], device_id={"tp": peer}, device_id_type=MESH)
 
     def phase0(stage):
-        return remote(0, stage, part.at[pl.ds(half - base0, half)], recv0.at[lax.rem(stage, 2)], partner)
-
-    def phase1(stage):
-        return remote(1, stage, sum0.at[lax.rem(stage, 2), pl.ds(quarter * (1 - pos1), quarter)], recv1.at[lax.rem(stage, 4)], first)
-
-    def phase2(stage):
-        return remote(2, stage, sum1.at[lax.rem(stage, 2), pl.ds(eighth * (1 - pos2), eighth)], recv2.at[lax.rem(stage, 4)], second)
-
-    def gather(phase, stage, start, size, peer):
+        return remote(0, stage, part.at[pl.ds(half - base, half)], recv0.at[lax.rem(stage, 2)], partner)
+
+    def phase1(stage, j):
+        block = pl.ds(quarter * j + eighth * (1 - pos1[j]), eighth)
+        return remote(1 + j, stage, sum0.at[lax.rem(stage, 2), block], recv1.at[lax.rem(stage, 4), pl.ds(eighth * j, eighth)], first[j])
+
+    def phase2(stage, j):
+        block = pl.ds(eighth * j + last * (1 - pos2[j]), last)
+        return remote(3 + j, stage, sum1.at[lax.rem(stage, 2), block], recv2.at[lax.rem(stage, 4), pl.ds(last * j, last)], second[j])
+
+    def gather(kind, stage, start, size, peer):
         block = hid.at[lax.rem(stage, n_chunks), pl.ds(start, size)]
-        return remote(phase, stage, block, block, peer)
-
-    def phase3(stage):
-        return gather(3, stage, base2, eighth, second)
-
-    def phase4(stage):
-        return gather(4, stage, base1, quarter, first)
+        return remote(kind, stage, block, block, peer)
+
+    def phase3(stage, j):
+        return gather(5 + j, stage, base2[j], last, second[j])
+
+    def phase4(stage, j):
+        return gather(7 + j, stage, base1[j], eighth, first[j])
 
     def phase5(stage):
-        return gather(5, stage, base0, half, partner)
+        return gather(9, stage, base, half, partner)
 
     barrier = pltpu.get_barrier_semaphore()
     for peer in (partner, x_peer, y_peer):
@@ -242,45 +241,46 @@
         def _():
             s = i - 1
             phase0(s).wait()
-
-            @pl.loop(0, half // 4)
-            def _(g):
-                ts = pl.ds(g * 4, 4)
-                sum0[lax.rem(s, 2), ts] = part[pl.ds(base0 + g * 4, 4)] + recv0[lax.rem(s, 2), ts]
-
-            phase1(s).start()
+            for j in range(2):
+                @pl.loop(0, quarter // 4)
+                def _(g):
+                    ts = pl.ds(quarter * j + g * 4, 4)
+                    sum0[lax.rem(s, 2), ts] = part[pl.ds(base + quarter * j + g * 4, 4)] + recv0[lax.rem(s, 2), ts]
+
+                phase1(s, j).start()
 
         @pl.when(between(i, 2))
         def _():
             s = i - 2
-            phase1(s).wait()
-
-            @pl.loop(0, quarter // 4)
-            def _(g):
-                ts = pl.ds(g * 4, 4)
-                sum1[lax.rem(s, 2), ts] = sum0[lax.rem(s, 2), pl.ds(quarter * pos1 + g * 4, 4)] + recv1[lax.rem(s, 4), ts]
-
-            phase2(s).start()
+            for j in range(2):
+                phase1(s, j).wait()
+                mine = pl.ds(quarter * j + eighth * pos1[j], eighth)
+                ts = pl.ds(eighth * j, eighth)
+                sum1[lax.rem(s, 2), ts] = sum0[lax.rem(s, 2), mine] + recv1[lax.rem(s, 4), ts]
+                phase2(s, j).start()
 
         @pl.when(between(i, 3))
         def _():
             s = i - 3
             where = lax.rem(s, n_chunks)
-            phase2(s).wait()
-            own = pl.ds(base2, eighth)
-            total = sum1[lax.rem(s, 2), pl.ds(eighth * pos2, eighth)].astype(F32) + recv2[lax.rem(s, 4)].astype(F32)
-            total = total + hid[where, own].astype(F32) + b_out[lax.div(s, n_chunks)][None]
-            hid[where, own] = total.astype(BF16)
-            phase3(s).start()
+            for j in range(2):
+                phase2(s, j).wait()
+                own = pl.ds(base2[j], last)
+                total = sum1[lax.rem(s, 2), pl.ds(eighth * j + last * pos2[j], last)].astype(F32) + recv2[lax.rem(s, 4), pl.ds(last * j, last)].astype(F32)
+                total = total + hid[where, own].astype(F32) + b_out[lax.div(s, n_chunks)][None]
+                hid[where, own] = total.astype(BF16)
+                phase3(s, j).start()
 
         @pl.when(between(i, 4))
         def _():
-            phase3(i - 4).wait()
-            phase4(i - 4).start()
+            for j in range(2):
+                phase3(i - 4, j).wait()
+                phase4(i - 4, j).start()
 
         @pl.when(between(i, 5))
         def _():
-            phase4(i - 5).wait()
+            for j in range(2):
+                phase4(i - 5, j).wait()
             phase5(i - 5).start()
 
         @pl.when(live)
@@ -383,7 +383,7 @@
             pltpu.VMEM((batch, cache_len * n_heads), jnp.int32), pltpu.VMEM((batch, 128), F32), pltpu.VMEM((batch, 128), F32),
             pltpu.VMEM((n_layers, 1, d_model), F32), pltpu.VMEM((n_layers, 1, d_model), F32),
             pltpu.VMEM((n_layers, 1, ff), F32), pltpu.VMEM((n_layers, 1, d_model), F32),
-            dma((n_layers, 6)), dma((n_chunks,)), dma((2, 2)), dma((2, 2)), dma((n_chunks,)), dma((6, 2)), dma((6, 4)),
+            dma((n_layers, 6)), dma((n_chunks,)), dma((2, 2)), dma((2, 2)), dma((n_chunks,)), dma((10, 2)), dma((10, 4)),
         ],
         compiler_params=pltpu.CompilerParams(collective_id=0, has_side_effects=True, vmem_limit_bytes=60 * 1024 * 1024),
         name="decode",

time: 198 us -> 192 us (0.970)
  Pallas kernels: 197 us -> 191 us
    pallas_call x1, Pallas kernels: 177 us -> 171 us  [decode_shard(): pl.pallas_call(functools.partial(decode_kernel, n_chunks, n_stages), out_...]
where the time goes in v6:
time: 192 us
  Pallas kernels  191 us (99%)
    pallas_call x1, Pallas kernels, decode_shard(): pl.pallas_call(functools.partial(decode_kernel, n_chunks, n_stages), out_...  171 us
    pallas_call x1, Pallas kernels, decode_shard(): pl.pallas_call(functools.partial(merge_kernel, n_blocks), out_shape=(jax....  20.4 us

profile of v6, /device:TPU:0, one launch (start us, length us, event | category | flops | bytes accessed | tf_op | source)
XLA Modules:
  0.0 192.0 jit_solution(4382076406081223679)
XLA Ops:
  0.6 170.9 %decode.1 = (bf16[32,64,2048]{2,1,0:T(8,128)(2,1)}, bf16[2,64,64,128]{3,2,1,0:T(8,128)(2,1)}, bf16[2,64,64,128]{3,2,1,0:T(8,128)(2,1)}) custom-call(bf16[32,64,2048]{2,1,0:T(8,128)(2,1)} %x_hbm.1, bf16[2,64,256,128]{3,2,1,0:T(8,128)(2,1)} %bitcast.8, bf16[2,64,256,128]{3,2,1,0:T(8,128)(2,1)} %bitcast.10, bf16[2,2048,256]{2,1,0:T(8,128)(2,1)} %wq_hbm.1, ...), custom_call_target="tpu_custom_call" | custom-call | tf_op jit(solution)/shard_map/decode/pallas_call | solution.py:364
  171.5 20.4 %merge.1 = (bf16[32,64,2048]{2,1,0:T(8,128)(2,1)}, bf16[128,128,2,128]{3,2,1,0:T(2,128)(2,1)}, bf16[128,128,2,128]{3,2,1,0:T(2,128)(2,1)}) custom-call(s32[64]{0:T(128)} %lens.1, bf16[32,64,2048]{2,1,0:T(8,128)(2,1)} %get-tuple-element.9.hid_in, bf16[128,128,2,128]{3,2,1,0:T(2,128)(2,1)} %bitcast.9, bf16[128,128,2,128]{3,2,1,0:T(2,128)(2,1)} %bitcast.11, ...), custom_call_target="tpu_custom_call" | custom-call | tf_op jit(solution)/shard_map/merge/pallas_call | solution.py:397

commit v7 on v6

--- a/solution.py
+++ b/solution.py
@@ -225,6 +225,20 @@
         def _():
             norm_and_project(i, layer, chunk)
 
+        @pl.when(between(i, 5))
+        def _():
+            for j in range(2):
+                phase3(i - 5, j).wait()
+                phase4(i - 5, j).start()
+
+        @pl.when(between(i, 6))
+        def _():
+            for j in range(2):
+                phase4(i - 6, j).wait()
+            phase5(i - 6).start()
+
+        @pl.when(live)
+        def _():
             @pl.when(i >= 1)
             def _():
                 for copy in rec_copies(i - 1):
@@ -249,6 +263,10 @@
 
                 phase1(s, j).start()
 
+        @pl.when(live)
+        def _():
+            feed_forward(layer, chunk)
+
         @pl.when(between(i, 2))
         def _():
             s = i - 2
@@ -258,6 +276,11 @@
                 ts = pl.ds(eighth * j, eighth)
                 sum1[lax.rem(s, 2), ts] = sum0[lax.rem(s, 2), mine] + recv1[lax.rem(s, 4), ts]
                 phase2(s, j).start()
+
+        @pl.when(live)
+        def _():
+            project_out(i, layer)
+            phase0(i).start()
 
         @pl.when(between(i, 3))
         def _():
@@ -271,27 +294,9 @@
                 hid[where, own] = total.astype(BF16)
                 phase3(s, j).start()
 
-        @pl.when(between(i, 4))
-        def _():
-            for j in range(2):
-                phase3(i - 4, j).wait()
-                phase4(i - 4, j).start()
-
-        @pl.when(between(i, 5))
-        def _():
-            for j in range(2):
-                phase4(i - 5, j).wait()
-            phase5(i - 5).start()
-
-        @pl.when(live)
-        def _():
-            feed_forward(layer, chunk)
-            project_out(i, layer)
-            phase0(i).start()
-
-        @pl.when(between(i, 5))
-        def _():
-            s = i - 5
+        @pl.when(between(i, 6))
+        def _():
+            s = i - 6
             phase5(s).wait()
 
             @pl.when(s >= n_stages - n_chunks)

time: 192 us -> 192 us (level)
  no operation moved by 1% of the time
where the time goes in v7:
time: 192 us
  Pallas kernels  191 us (99%)
    pallas_call x1, Pallas kernels, decode_shard(): pl.pallas_call(functools.partial(decode_kernel, n_chunks, n_stages), out_...  171 us
    pallas_call x1, Pallas kernels, decode_shard(): pl.pallas_call(functools.partial(merge_kernel, n_blocks), out_shape=(jax....  20.4 us

profile of v7, /device:TPU:0, one launch (start us, length us, event | category | flops | bytes accessed | tf_op | source)
XLA Modules:
  0.0 192.1 jit_solution(7479834086329458935)
XLA Ops:
  0.6 171.0 %decode.1 = (bf16[32,64,2048]{2,1,0:T(8,128)(2,1)}, bf16[2,64,64,128]{3,2,1,0:T(8,128)(2,1)}, bf16[2,64,64,128]{3,2,1,0:T(8,128)(2,1)}) custom-call(bf16[32,64,2048]{2,1,0:T(8,128)(2,1)} %x_hbm.1, bf16[2,64,256,128]{3,2,1,0:T(8,128)(2,1)} %bitcast.8, bf16[2,64,256,128]{3,2,1,0:T(8,128)(2,1)} %bitcast.10, bf16[2,2048,256]{2,1,0:T(8,128)(2,1)} %wq_hbm.1, ...), custom_call_target="tpu_custom_call" | custom-call | tf_op jit(solution)/shard_map/decode/pallas_call | solution.py:369
  171.7 20.4 %merge.1 = (bf16[32,64,2048]{2,1,0:T(8,128)(2,1)}, bf16[128,128,2,128]{3,2,1,0:T(2,128)(2,1)}, bf16[128,128,2,128]{3,2,1,0:T(2,128)(2,1)}) custom-call(s32[64]{0:T(128)} %lens.1, bf16[32,64,2048]{2,1,0:T(8,128)(2,1)} %get-tuple-element.9.hid_in, bf16[128,128,2,128]{3,2,1,0:T(2,128)(2,1)} %bitcast.9, bf16[128,128,2,128]{3,2,1,0:T(2,128)(2,1)} %bitcast.11, ...), custom_call_target="tpu_custom_call" | custom-call | tf_op jit(solution)/shard_map/merge/pallas_call | solution.py:402

commit v8 on v7

--- a/solution.py
+++ b/solution.py
@@ -21,11 +21,12 @@
                   lens_in, inv_freq, cos_t, sin_t, gain_in, bias_in, b_in_in, b_out_in,
                   out_hbm, rec_k, rec_v,
                   wq, wk, wv, wo, win, wout, hid, part, recv0, sum0, recv1, sum1, recv2,
-                  normed, qf, kf, vf, cf, ctx, act, inter, scores, kbuf, vbuf,
+                  normed, qf, kf, vf, cf, ctx, act, inter, scores, key_scr, kbuf, vbuf,
                   lens, cos_c, sin_c, gain, bias, b_in, b_out,
                   w_sem, x_sem, kv_sem, rec_sem, out_sem, send_sem, recv_sem):
     steps = x_hbm.shape[0]
     rows = steps * SEQS
+    ff = win_hbm.shape[2]
     half, quarter, eighth, last = steps // 2, steps // 4, steps // 8, steps // 16
     d_model = x_hbm.shape[2]
     me = lax.axis_index("tp")
@@ -119,22 +120,16 @@
             dst[layer] = src[layer:layer + 1, :].astype(F32)
     pl.semaphore_wait(barrier, 3)
 
-    def norm_and_project(stage, layer, chunk):
-        @pl.when(layer == 0)
-        def _():
-            x_copy(chunk).wait()
-
-        group = 8
-
-        @pl.loop(0, steps // group)
-        def _(g):
-            x = hid[chunk, pl.ds(g * group, group)].astype(F32)
-            mean = jnp.mean(x, axis=-1, keepdims=True)
-            centered = x - mean
+    def norm_rows(stage, start, count):
+        layer, chunk, slot = lax.div(stage, n_chunks), lax.rem(stage, n_chunks), lax.rem(stage, 2)
+        for k in range(0, count, 2):
+            x = hid[chunk, pl.ds(start + k, 2)].astype(F32)
+            centered = x - jnp.mean(x, axis=-1, keepdims=True)
             var = jnp.mean(centered * centered, axis=-1, keepdims=True)
             y = centered * lax.rsqrt(var + LN_EPS) * gain[layer][None] + bias[layer][None]
-            normed[pl.ds(pl.multiple_of(g * group * SEQS, group * SEQS), group * SEQS), :] = y.reshape(group * SEQS, d_model).astype(BF16)
-
+            normed[slot, pl.ds((start + k) * SEQS if isinstance(start, int) else pl.multiple_of((start + k) * SEQS, 2 * SEQS), 2 * SEQS), pl.ds(0, d_model)] = y.reshape(2 * SEQS, d_model).astype(BF16)
+
+    def project_in(stage, layer, chunk):
         @pl.when(chunk == 0)
         def _():
             for j in range(3):
@@ -148,7 +143,7 @@
         even = lax.rem(lax.broadcasted_iota(jnp.int32, (rows, 128), 1), 2) == 0
 
         for weight, dst, rotate in ((wq, qf, True), (wk, kf, True), (wv, vf, False)):
-            vec = jnp.dot(normed[...], weight[layer], preferred_element_type=F32)
+            vec = jnp.dot(normed[lax.rem(stage, 2), :, pl.ds(0, d_model)], weight[layer], preferred_element_type=F32)
             for h in range(2):
                 piece = vec[:, h * 128:(h + 1) * 128]
                 if rotate:
@@ -160,28 +155,31 @@
         slot = lax.rem(stage, 2)
         for copy in kv_copies(stage):
             copy.wait()
+
+        @pl.when(chunk == 0)
+        def _():
+            for j in range(3, 6):
+                weight_copy(layer, j).wait()
+
         shape = (2 * steps, 2 * (OLD + steps))
         row, col = lax.broadcasted_iota(jnp.int32, shape, 0), lax.broadcasted_iota(jnp.int32, shape, 1)
         col_slot, col_head = lax.shift_right_logical(col, 1), lax.bitwise_and(col, 1)
         row_head, row_step = lax.div(row, steps), lax.rem(row, steps)
         never = 1 << 20
         fresh = jnp.where(col_slot - OLD <= row_step, -1, never)
-        key = jnp.where(row_head == col_head, jnp.where(col_slot >= OLD, fresh, col_slot), never)
-        here = pl.ds(pl.multiple_of(chunk * SEQS, SEQS), SEQS)
-        limit = lens[here, :]
+        key_scr[...] = jnp.where(row_head == col_head, jnp.where(col_slot >= OLD, fresh, col_slot), never)
+        limit = lens[pl.ds(pl.multiple_of(chunk * SEQS, SEQS), SEQS), :]
         for b in range(SEQS):
             mine = pl.ds(b, steps, stride=SEQS)
             for src, buf, j in ((kf, kbuf, 0), (vf, vbuf, 1)):
                 for h in range(2):
                     inter[b, j, pl.ds(h, steps, stride=2), :] = src[h, mine, :]
                 buf[slot, b, pl.ds(2 * OLD, 2 * steps), :] = inter[b, j].astype(BF16)
-        for copy in rec_copies(stage):
-            copy.start()
         for b in range(SEQS):
             mine = pl.ds(b, steps, stride=SEQS)
             query = jnp.concatenate([qf[0, mine, :], qf[1, mine, :]], axis=0).astype(BF16)
             s = lax.dot_general(query, kbuf[slot, b], (((1,), (1,)), ((), ())), preferred_element_type=F32) * (128 ** -0.5)
-            scores[b] = jnp.where(key < limit[b:b + 1, :], s, -jnp.inf)
+            scores[b] = jnp.where(key_scr[...] < limit[b:b + 1, :], s, -jnp.inf)
         for b in range(SEQS):
             s = scores[b]
             e = jnp.exp(s - jnp.max(s, axis=-1, keepdims=True))
@@ -190,28 +188,39 @@
             for h in range(2):
                 cf[h, pl.ds(b, steps, stride=SEQS), :] = context[h * steps:(h + 1) * steps]
 
-    def feed_forward(layer, chunk):
-        @pl.when(chunk == 0)
-        def _():
-            for j in range(3, 6):
-                weight_copy(layer, j).wait()
-
-        @pl.loop(0, act.shape[1] // 256, unroll=2)
-        def _(n):
-            cols = pl.ds(pl.multiple_of(n * 256, 256), 256)
-            pre = jnp.dot(normed[...], win[layer, :, cols], preferred_element_type=F32) + b_in[layer, :, cols]
+        for copy in rec_copies(stage):
+            copy.start()
+
+    def feed_forward(stage, layer):
+        slot = lax.rem(stage, 2)
+        for n in range(ff // 256):
+            cols = pl.ds(n * 256, 256)
+            pre = jnp.dot(normed[slot, :, pl.ds(0, d_model)], win[layer, :, cols], preferred_element_type=F32) + b_in[layer, :, cols]
             act[:, cols] = jax.nn.gelu(pre, approximate=True).astype(BF16)
 
     def project_out(stage, layer):
         for h in range(2):
             ctx[:, h * 128:(h + 1) * 128] = cf[h].astype(BF16)
 
-        @pl.loop(0, d_model // 256, unroll=2)
-        def _(n):
-            cols = pl.ds(pl.multiple_of(n * 256, 256), 256)
+        following = jnp.minimum(stage + 1, n_stages - 1)
+        group = steps // (d_model // 256)
+
+        @pl.when(stage + 1 < n_chunks)
+        def _():
+            x_copy(stage + 1).wait()
+
+        for n in range(d_model // 256):
+            cols = pl.ds(n * 256, 256)
             total = jnp.dot(ctx[...], wo[layer, :, cols], preferred_element_type=F32)
-            total += jnp.dot(act[...], wout[layer, :, cols], preferred_element_type=F32)
+            total += jnp.dot(act[:, pl.ds(0, ff)], wout[layer, :, cols], preferred_element_type=F32)
             part[:, :, cols] = total.reshape(steps, SEQS, 256).astype(BF16)
+            norm_rows(following, n * group, group)
+
+    x_copy(0).wait()
+
+    @pl.loop(0, steps // 8)
+    def _(g):
+        norm_rows(0, g * 8, 8)
 
     def between(i, lag):
         return jnp.logical_and(i >= lag, i < n_stages + lag)
@@ -223,7 +232,7 @@
 
         @pl.when(live)
         def _():
-            norm_and_project(i, layer, chunk)
+            project_in(i, layer, chunk)
 
         @pl.when(between(i, 5))
         def _():
@@ -265,7 +274,7 @@
 
         @pl.when(live)
         def _():
-            feed_forward(layer, chunk)
+            feed_forward(i, layer)
 
         @pl.when(between(i, 2))
         def _():
@@ -380,10 +389,10 @@
             pltpu.VMEM((2, steps // 2, SEQS, d_model), BF16), pltpu.VMEM((2, steps // 2, SEQS, d_model), BF16),
             pltpu.VMEM((4, steps // 4, SEQS, d_model), BF16), pltpu.VMEM((2, steps // 4, SEQS, d_model), BF16),
             pltpu.VMEM((4, steps // 8, SEQS, d_model), BF16),
-            pltpu.VMEM((rows, d_model), BF16),
+            pltpu.VMEM((2, rows, d_model + 128), BF16),
             pltpu.VMEM((2, rows, 128), F32), pltpu.VMEM((2, rows, 128), F32), pltpu.VMEM((2, rows, 128), F32), pltpu.VMEM((2, rows, 128), F32),
-            pltpu.VMEM((rows, 256), BF16), pltpu.VMEM((rows, ff), BF16),
-            pltpu.VMEM((SEQS, 2, 2 * steps, 128), F32), pltpu.VMEM((SEQS, 2 * steps, 256), F32),
+            pltpu.VMEM((rows, 256), BF16), pltpu.VMEM((rows, ff + 128), BF16),
+            pltpu.VMEM((SEQS, 2, 2 * steps, 128), F32), pltpu.VMEM((SEQS, 2 * steps, 256), F32), pltpu.VMEM((2 * steps, 256), jnp.int32),
             pltpu.VMEM((2, SEQS, 256, 128), BF16), pltpu.VMEM((2, SEQS, 256, 128), BF16),
             pltpu.VMEM((batch, cache_len * n_heads), jnp.int32), pltpu.VMEM((batch, 128), F32), pltpu.VMEM((batch, 128), F32),
             pltpu.VMEM((n_layers, 1, d_model), F32), pltpu.VMEM((n_layers, 1, d_model), F32),

time: 192 us -> 185 us (0.964)
  Pallas kernels: 191 us -> 184 us
    pallas_call x1, Pallas kernels: 171 us -> 164 us  [decode_shard(): pl.pallas_call(functools.partial(decode_kernel, n_chunks, n_stages), out_...]
where the time goes in v8:
time: 185 us
  Pallas kernels  184 us (99%)
    pallas_call x1, Pallas kernels, decode_shard(): pl.pallas_call(functools.partial(decode_kernel, n_chunks, n_stages), out_...  164 us
    pallas_call x1, Pallas kernels, decode_shard(): pl.pallas_call(functools.partial(merge_kernel, n_blocks), out_shape=(jax....  20.4 us

profile of v8, /device:TPU:0, one launch (start us, length us, event | category | flops | bytes accessed | tf_op | source)
XLA Modules:
  0.0 184.6 jit_solution(7461991069287130989)
XLA Ops:
  0.6 163.5 %decode.1 = (bf16[32,64,2048]{2,1,0:T(8,128)(2,1)}, bf16[2,64,64,128]{3,2,1,0:T(8,128)(2,1)}, bf16[2,64,64,128]{3,2,1,0:T(8,128)(2,1)}) custom-call(bf16[32,64,2048]{2,1,0:T(8,128)(2,1)} %x_hbm.1, bf16[2,64,256,128]{3,2,1,0:T(8,128)(2,1)} %bitcast.8, bf16[2,64,256,128]{3,2,1,0:T(8,128)(2,1)} %bitcast.10, bf16[2,2048,256]{2,1,0:T(8,128)(2,1)} %wq_hbm.1, ...), custom_call_target="tpu_custom_call" | custom-call | tf_op jit(solution)/shard_map/decode/pallas_call | solution.py:378
  164.2 20.4 %merge.1 = (bf16[32,64,2048]{2,1,0:T(8,128)(2,1)}, bf16[128,128,2,128]{3,2,1,0:T(2,128)(2,1)}, bf16[128,128,2,128]{3,2,1,0:T(2,128)(2,1)}) custom-call(s32[64]{0:T(128)} %lens.1, bf16[32,64,2048]{2,1,0:T(8,128)(2,1)} %get-tuple-element.9.hid_in, bf16[128,128,2,128]{3,2,1,0:T(2,128)(2,1)} %bitcast.9, bf16[128,128,2,128]{3,2,1,0:T(2,128)(2,1)} %bitcast.11, ...), custom_call_target="tpu_custom_call" | custom-call | tf_op jit(solution)/shard_map/merge/pallas_call | solution.py:411

commit v9 on v8

--- a/solution.py
+++ b/solution.py
@@ -105,10 +105,7 @@
         copy.start()
     for j in range(3, 6):
         weight_copy(0, j).start()
-    for chunk in range(1, n_chunks):
-        x_copy(chunk).start()
-    for j in range(6):
-        weight_copy(1, j).start()
+    x_copy(1).start()
     for b in range(lens.shape[0]):
         lens[b:b + 1, :] = jnp.full((1, lens.shape[1]), lens_in[b], jnp.int32)
     angles = lens[:, 0:128].astype(F32) * inv_freq[...]
@@ -118,7 +115,6 @@
     for src, dst in ((gain_in, gain), (bias_in, bias), (b_in_in, b_in), (b_out_in, b_out)):
         for layer in range(src.shape[0]):
             dst[layer] = src[layer:layer + 1, :].astype(F32)
-    pl.semaphore_wait(barrier, 3)
 
     def norm_rows(stage, start, count):
         layer, chunk, slot = lax.div(stage, n_chunks), lax.rem(stage, n_chunks), lax.rem(stage, 2)
@@ -222,14 +218,23 @@
     def _(g):
         norm_rows(0, g * 8, 8)
 
+    pl.semaphore_wait(barrier, 3)
+
     def between(i, lag):
         return jnp.logical_and(i >= lag, i < n_stages + lag)
 
-    @pl.loop(0, n_stages + 6)
+    @pl.loop(0, n_stages + 7)
     def _(i):
         layer, chunk = lax.div(i, n_chunks), lax.rem(i, n_chunks)
         live = i < n_stages
 
+        @pl.when(i == 1)
+        def _():
+            for c in range(2, n_chunks):
+                x_copy(c).start()
+            for j in range(6):
+                weight_copy(1, j).start()
+
         @pl.when(live)
         def _():
             project_in(i, layer, chunk)
@@ -239,6 +244,15 @@
             for j in range(2):
                 phase3(i - 5, j).wait()
                 phase4(i - 5, j).start()
+
+        @pl.when(between(i, 7))
+        def _():
+            s = i - 7
+            phase5(s).wait()
+
+            @pl.when(s >= n_stages - n_chunks)
+            def _():
+                out_copy(lax.rem(s, n_chunks)).start()
 
         @pl.when(between(i, 6))
         def _():
@@ -302,15 +316,6 @@
                 total = total + hid[where, own].astype(F32) + b_out[lax.div(s, n_chunks)][None]
                 hid[where, own] = total.astype(BF16)
                 phase3(s, j).start()
-
-        @pl.when(between(i, 6))
-        def _():
-            s = i - 6
-            phase5(s).wait()
-
-            @pl.when(s >= n_stages - n_chunks)
-            def _():
-                out_copy(lax.rem(s, n_chunks)).start()
 
     for copy in rec_copies(n_stages - 1):
         copy.wait()

time: 185 us -> 181 us (0.978)
  Pallas kernels: 184 us -> 180 us
    pallas_call x1, Pallas kernels: 164 us -> 159 us  [decode_shard(): pl.pallas_call(functools.partial(decode_kernel, n_chunks, n_stages), out_...]
where the time goes in v9:
time: 181 us; the launch traced here: 180 us
  Pallas kernels  180 us (99%)
    pallas_call x1, Pallas kernels, decode_shard(): pl.pallas_call(functools.partial(decode_kernel, n_chunks, n_stages), out_...  159 us
    pallas_call x1, Pallas kernels, decode_shard(): pl.pallas_call(functools.partial(merge_kernel, n_blocks), out_shape=(jax....  20.4 us

profile of v9, /device:TPU:0, one launch (start us, length us, event | category | flops | bytes accessed | tf_op | source)
XLA Modules:
  0.0 180.5 jit_solution(15338128748503997529)
XLA Ops:
  0.6 159.4 %decode.1 = (bf16[32,64,2048]{2,1,0:T(8,128)(2,1)}, bf16[2,64,64,128]{3,2,1,0:T(8,128)(2,1)}, bf16[2,64,64,128]{3,2,1,0:T(8,128)(2,1)}) custom-call(bf16[32,64,2048]{2,1,0:T(8,128)(2,1)} %x_hbm.1, bf16[2,64,256,128]{3,2,1,0:T(8,128)(2,1)} %bitcast.8, bf16[2,64,256,128]{3,2,1,0:T(8,128)(2,1)} %bitcast.10, bf16[2,2048,256]{2,1,0:T(8,128)(2,1)} %wq_hbm.1, ...), custom_call_target="tpu_custom_call" | custom-call | tf_op jit(solution)/shard_map/decode/pallas_call | solution.py:383
  160.1 20.4 %merge.1 = (bf16[32,64,2048]{2,1,0:T(8,128)(2,1)}, bf16[128,128,2,128]{3,2,1,0:T(2,128)(2,1)}, bf16[128,128,2,128]{3,2,1,0:T(2,128)(2,1)}) custom-call(s32[64]{0:T(128)} %lens.1, bf16[32,64,2048]{2,1,0:T(8,128)(2,1)} %get-tuple-element.9.hid_in, bf16[128,128,2,128]{3,2,1,0:T(2,128)(2,1)} %bitcast.9, bf16[128,128,2,128]{3,2,1,0:T(2,128)(2,1)} %bitcast.11, ...), custom_call_target="tpu_custom_call" | custom-call | tf_op jit(solution)/shard_map/merge/pallas_call | solution.py:416

commit v10 on v9

--- a/solution.py
+++ b/solution.py
@@ -223,7 +223,7 @@
     def between(i, lag):
         return jnp.logical_and(i >= lag, i < n_stages + lag)
 
-    @pl.loop(0, n_stages + 7)
+    @pl.loop(0, n_stages + 5)
     def _(i):
         layer, chunk = lax.div(i, n_chunks), lax.rem(i, n_chunks)
         live = i < n_stages
@@ -239,26 +239,24 @@
         def _():
             project_in(i, layer, chunk)
 
+        @pl.when(between(i, 2))
+        def _():
+            s = i - 2
+            for j in range(2):
+                phase1(s, j).wait()
+                mine = pl.ds(quarter * j + eighth * pos1[j], eighth)
+                ts = pl.ds(eighth * j, eighth)
+                sum1[lax.rem(s, 2), ts] = sum0[lax.rem(s, 2), mine] + recv1[lax.rem(s, 4), ts]
+                phase2(s, j).start()
+
         @pl.when(between(i, 5))
         def _():
-            for j in range(2):
-                phase3(i - 5, j).wait()
-                phase4(i - 5, j).start()
-
-        @pl.when(between(i, 7))
-        def _():
-            s = i - 7
+            s = i - 5
             phase5(s).wait()
 
             @pl.when(s >= n_stages - n_chunks)
             def _():
                 out_copy(lax.rem(s, n_chunks)).start()
-
-        @pl.when(between(i, 6))
-        def _():
-            for j in range(2):
-                phase4(i - 6, j).wait()
-            phase5(i - 6).start()
 
         @pl.when(live)
         def _():
@@ -290,24 +288,26 @@
         def _():
             feed_forward(i, layer)
 
-        @pl.when(between(i, 2))
-        def _():
-            s = i - 2
+        @pl.when(between(i, 3))
+        def _():
             for j in range(2):
-                phase1(s, j).wait()
-                mine = pl.ds(quarter * j + eighth * pos1[j], eighth)
-                ts = pl.ds(eighth * j, eighth)
-                sum1[lax.rem(s, 2), ts] = sum0[lax.rem(s, 2), mine] + recv1[lax.rem(s, 4), ts]
-                phase2(s, j).start()
+                phase3(i - 3, j).wait()
+                phase4(i - 3, j).start()
+
+        @pl.when(between(i, 4))
+        def _():
+            for j in range(2):
+                phase4(i - 4, j).wait()
+            phase5(i - 4).start()
 
         @pl.when(live)
         def _():
             project_out(i, layer)
             phase0(i).start()
 
-        @pl.when(between(i, 3))
-        def _():
-            s = i - 3
+        @pl.when(between(i, 2))
+        def _():
+            s = i - 2
             where = lax.rem(s, n_chunks)
             for j in range(2):
                 phase2(s, j).wait()

time: 181 us -> 180 us (level)
  no operation moved by 1% of the time
where the time goes in v10:
time: 180 us
  Pallas kernels  180 us (100%)
    pallas_call x1, Pallas kernels, decode_shard(): pl.pallas_call(functools.partial(decode_kernel, n_chunks, n_stages), out_...  159 us
    pallas_call x1, Pallas kernels, decode_shard(): pl.pallas_call(functools.partial(merge_kernel, n_blocks), out_shape=(jax....  20.4 us

profile of v10, /device:TPU:0, one launch (start us, length us, event | category | flops | bytes accessed | tf_op | source)
XLA Modules:
  0.0 180.2 jit_solution(1891346651258217475)
XLA Ops:
  0.6 159.1 %decode.1 = (bf16[32,64,2048]{2,1,0:T(8,128)(2,1)}, bf16[2,64,64,128]{3,2,1,0:T(8,128)(2,1)}, bf16[2,64,64,128]{3,2,1,0:T(8,128)(2,1)}) custom-call(bf16[32,64,2048]{2,1,0:T(8,128)(2,1)} %x_hbm.1, bf16[2,64,256,128]{3,2,1,0:T(8,128)(2,1)} %bitcast.8, bf16[2,64,256,128]{3,2,1,0:T(8,128)(2,1)} %bitcast.10, bf16[2,2048,256]{2,1,0:T(8,128)(2,1)} %wq_hbm.1, ...), custom_call_target="tpu_custom_call" | custom-call | tf_op jit(solution)/shard_map/decode/pallas_call | solution.py:383
  159.8 20.4 %merge.1 = (bf16[32,64,2048]{2,1,0:T(8,128)(2,1)}, bf16[128,128,2,128]{3,2,1,0:T(2,128)(2,1)}, bf16[128,128,2,128]{3,2,1,0:T(2,128)(2,1)}) custom-call(s32[64]{0:T(128)} %lens.1, bf16[32,64,2048]{2,1,0:T(8,128)(2,1)} %get-tuple-element.9.hid_in, bf16[128,128,2,128]{3,2,1,0:T(2,128)(2,1)} %bitcast.9, bf16[128,128,2,128]{3,2,1,0:T(2,128)(2,1)} %bitcast.11, ...), custom_call_target="tpu_custom_call" | custom-call | tf_op jit(solution)/shard_map/merge/pallas_call | solution.py:416

commit v11 on v10

--- a/solution.py
+++ b/solution.py
@@ -239,75 +239,9 @@
         def _():
             project_in(i, layer, chunk)
 
-        @pl.when(between(i, 2))
-        def _():
-            s = i - 2
-            for j in range(2):
-                phase1(s, j).wait()
-                mine = pl.ds(quarter * j + eighth * pos1[j], eighth)
-                ts = pl.ds(eighth * j, eighth)
-                sum1[lax.rem(s, 2), ts] = sum0[lax.rem(s, 2), mine] + recv1[lax.rem(s, 4), ts]
-                phase2(s, j).start()
-
-        @pl.when(between(i, 5))
-        def _():
-            s = i - 5
-            phase5(s).wait()
-
-            @pl.when(s >= n_stages - n_chunks)
-            def _():
-                out_copy(lax.rem(s, n_chunks)).start()
-
-        @pl.when(live)
-        def _():
-            @pl.when(i >= 1)
-            def _():
-                for copy in rec_copies(i - 1):
-                    copy.wait()
-
-            @pl.when(i + 1 < n_stages)
-            def _():
-                for copy in kv_copies(i + 1):
-                    copy.start()
-
-            attend(i, layer, chunk)
-
-        @pl.when(between(i, 1))
-        def _():
-            s = i - 1
-            phase0(s).wait()
-            for j in range(2):
-                @pl.loop(0, quarter // 4)
-                def _(g):
-                    ts = pl.ds(quarter * j + g * 4, 4)
-                    sum0[lax.rem(s, 2), ts] = part[pl.ds(base + quarter * j + g * 4, 4)] + recv0[lax.rem(s, 2), ts]
-
-                phase1(s, j).start()
-
-        @pl.when(live)
-        def _():
-            feed_forward(i, layer)
-
         @pl.when(between(i, 3))
         def _():
-            for j in range(2):
-                phase3(i - 3, j).wait()
-                phase4(i - 3, j).start()
-
-        @pl.when(between(i, 4))
-        def _():
-            for j in range(2):
-                phase4(i - 4, j).wait()
-            phase5(i - 4).start()
-
-        @pl.when(live)
-        def _():
-            project_out(i, layer)
-            phase0(i).start()
-
-        @pl.when(between(i, 2))
-        def _():
-            s = i - 2
+            s = i - 3
             where = lax.rem(s, n_chunks)
             for j in range(2):
                 phase2(s, j).wait()
@@ -316,6 +250,72 @@
                 total = total + hid[where, own].astype(F32) + b_out[lax.div(s, n_chunks)][None]
                 hid[where, own] = total.astype(BF16)
                 phase3(s, j).start()
+
+        @pl.when(live)
+        def _():
+            @pl.when(i >= 1)
+            def _():
+                for copy in rec_copies(i - 1):
+                    copy.wait()
+
+            @pl.when(i + 1 < n_stages)
+            def _():
+                for copy in kv_copies(i + 1):
+                    copy.start()
+
+            attend(i, layer, chunk)
+
+        @pl.when(between(i, 2))
+        def _():
+            s = i - 2
+            for j in range(2):
+                phase1(s, j).wait()
+                mine = pl.ds(quarter * j + eighth * pos1[j], eighth)
+                ts = pl.ds(eighth * j, eighth)
+                sum1[lax.rem(s, 2), ts] = sum0[lax.rem(s, 2), mine] + recv1[lax.rem(s, 4), ts]
+                phase2(s, j).start()
+
+        @pl.when(live)
+        def _():
+            feed_forward(i, layer)
+
+        @pl.when(between(i, 1))
+        def _():
+            s = i - 1
+            phase0(s).wait()
+            for j in range(2):
+                @pl.loop(0, quarter // 4)
+                def _(g):
+                    ts = pl.ds(quarter * j + g * 4, 4)
+                    sum0[lax.rem(s, 2), ts] = part[pl.ds(base + quarter * j + g * 4, 4)] + recv0[lax.rem(s, 2), ts]
+
+                phase1(s, j).start()
+
+        @pl.when(between(i, 5))
+        def _():
+            s = i - 5
+            phase5(s).wait()
+
+            @pl.when(s >= n_stages - n_chunks)
+            def _():
+                out_copy(lax.rem(s, n_chunks)).start()
+
+        @pl.when(live)
+        def _():
+            project_out(i, layer)
+            phase0(i).start()
+
+        @pl.when(between(i, 3))
+        def _():
+            for j in range(2):
+                phase3(i - 3, j).wait()
+                phase4(i - 3, j).start()
+
+        @pl.when(between(i, 4))
+        def _():
+            for j in range(2):
+                phase4(i - 4, j).wait()
+            phase5(i - 4).start()
 
     for copy in rec_copies(n_stages - 1):
         copy.wait()

time: 180 us -> 182 us (1.011)
  Pallas kernels: 180 us -> 182 us
    pallas_call x1, Pallas kernels: 159 us -> 161 us  [decode_shard(): pl.pallas_call(functools.partial(decode_kernel, n_chunks, n_stages), out_...]
where the time goes in v11:
time: 182 us
  Pallas kernels  182 us (100%)
    pallas_call x1, Pallas kernels, decode_shard(): pl.pallas_call(functools.partial(decode_kernel, n_chunks, n_stages), out_...  161 us
    pallas_call x1, Pallas kernels, decode_shard(): pl.pallas_call(functools.partial(merge_kernel, n_blocks), out_shape=(jax....  20.4 us

profile of v11, /device:TPU:0, one launch (start us, length us, event | category | flops | bytes accessed | tf_op | source)
XLA Modules:
  0.0 182.4 jit_solution(17642339680032350114)
XLA Ops:
  0.6 161.3 %decode.1 = (bf16[32,64,2048]{2,1,0:T(8,128)(2,1)}, bf16[2,64,64,128]{3,2,1,0:T(8,128)(2,1)}, bf16[2,64,64,128]{3,2,1,0:T(8,128)(2,1)}) custom-call(bf16[32,64,2048]{2,1,0:T(8,128)(2,1)} %x_hbm.1, bf16[2,64,256,128]{3,2,1,0:T(8,128)(2,1)} %bitcast.8, bf16[2,64,256,128]{3,2,1,0:T(8,128)(2,1)} %bitcast.10, bf16[2,2048,256]{2,1,0:T(8,128)(2,1)} %wq_hbm.1, ...), custom_call_target="tpu_custom_call" | custom-call | tf_op jit(solution)/shard_map/decode/pallas_call | solution.py:383
  161.9 20.4 %merge.1 = (bf16[32,64,2048]{2,1,0:T(8,128)(2,1)}, bf16[128,128,2,128]{3,2,1,0:T(2,128)(2,1)}, bf16[128,128,2,128]{3,2,1,0:T(2,128)(2,1)}) custom-call(s32[64]{0:T(128)} %lens.1, bf16[32,64,2048]{2,1,0:T(8,128)(2,1)} %get-tuple-element.9.hid_in, bf16[128,128,2,128]{3,2,1,0:T(2,128)(2,1)} %bitcast.9, bf16[128,128,2,128]{3,2,1,0:T(2,128)(2,1)} %bitcast.11, ...), custom_call_target="tpu_custom_call" | custom-call | tf_op jit(solution)/shard_map/merge/pallas_call | solution.py:416

commit v12 on v10

--- a/solution.py
+++ b/solution.py
@@ -101,11 +101,6 @@
     x_copy(0).start()
     for j in range(3):
         weight_copy(0, j).start()
-    for copy in kv_copies(0):
-        copy.start()
-    for j in range(3, 6):
-        weight_copy(0, j).start()
-    x_copy(1).start()
     for b in range(lens.shape[0]):
         lens[b:b + 1, :] = jnp.full((1, lens.shape[1]), lens_in[b], jnp.int32)
     angles = lens[:, 0:128].astype(F32) * inv_freq[...]
@@ -213,6 +208,11 @@
             norm_rows(following, n * group, group)
 
     x_copy(0).wait()
+    for copy in kv_copies(0):
+        copy.start()
+    for j in range(3, 6):
+        weight_copy(0, j).start()
+    x_copy(1).start()
 
     @pl.loop(0, steps // 8)
     def _(g):
@@ -228,11 +228,13 @@
         layer, chunk = lax.div(i, n_chunks), lax.rem(i, n_chunks)
         live = i < n_stages
 
-        @pl.when(i == 1)
-        def _():
-            for c in range(2, n_chunks):
-                x_copy(c).start()
-            for j in range(6):
+        @pl.when(i + 2 < n_chunks)
+        def _():
+            x_copy(i + 2).start()
+
+        for j in range(6):
+            @pl.when(i == j + 1)
+            def _():
                 weight_copy(1, j).start()
 
         @pl.when(live)

time: 180 us -> 180 us (level)
  no operation moved by 1% of the time
where the time goes in v12:
time: 180 us
  Pallas kernels  180 us (100%)
    pallas_call x1, Pallas kernels, decode_shard(): pl.pallas_call(functools.partial(decode_kernel, n_chunks, n_stages), out_...  159 us
    pallas_call x1, Pallas kernels, decode_shard(): pl.pallas_call(functools.partial(merge_kernel, n_blocks), out_shape=(jax....  20.4 us

profile of v12, /device:TPU:0, one launch (start us, length us, event | category | flops | bytes accessed | tf_op | source)
XLA Modules:
  0.0 180.2 jit_solution(8461110278805764945)
XLA Ops:
  0.6 159.1 %decode.1 = (bf16[32,64,2048]{2,1,0:T(8,128)(2,1)}, bf16[2,64,64,128]{3,2,1,0:T(8,128)(2,1)}, bf16[2,64,64,128]{3,2,1,0:T(8,128)(2,1)}) custom-call(bf16[32,64,2048]{2,1,0:T(8,128)(2,1)} %x_hbm.1, bf16[2,64,256,128]{3,2,1,0:T(8,128)(2,1)} %bitcast.8, bf16[2,64,256,128]{3,2,1,0:T(8,128)(2,1)} %bitcast.10, bf16[2,2048,256]{2,1,0:T(8,128)(2,1)} %wq_hbm.1, ...), custom_call_target="tpu_custom_call" | custom-call | tf_op jit(solution)/shard_map/decode/pallas_call | solution.py:385
  159.8 20.4 %merge.1 = (bf16[32,64,2048]{2,1,0:T(8,128)(2,1)}, bf16[128,128,2,128]{3,2,1,0:T(2,128)(2,1)}, bf16[128,128,2,128]{3,2,1,0:T(2,128)(2,1)}) custom-call(s32[64]{0:T(128)} %lens.1, bf16[32,64,2048]{2,1,0:T(8,128)(2,1)} %get-tuple-element.9.hid_in, bf16[128,128,2,128]{3,2,1,0:T(2,128)(2,1)} %bitcast.9, bf16[128,128,2,128]{3,2,1,0:T(2,128)(2,1)} %bitcast.11, ...), custom_call_target="tpu_custom_call" | custom-call | tf_op jit(solution)/shard_map/merge/pallas_call | solution.py:418

commit v13 on v12

--- a/solution.py
+++ b/solution.py
@@ -241,6 +241,18 @@
         def _():
             project_in(i, layer, chunk)
 
+        @pl.when(between(i, 1))
+        def _():
+            s = i - 1
+            phase0(s).wait()
+            for j in range(2):
+                @pl.loop(0, quarter // 4)
+                def _(g):
+                    ts = pl.ds(quarter * j + g * 4, 4)
+                    sum0[lax.rem(s, 2), ts] = part[pl.ds(base + quarter * j + g * 4, 4)] + recv0[lax.rem(s, 2), ts]
+
+                phase1(s, j).start()
+
         @pl.when(between(i, 2))
         def _():
             s = i - 2
@@ -273,18 +285,6 @@
                     copy.start()
 
             attend(i, layer, chunk)
-
-        @pl.when(between(i, 1))
-        def _():
-            s = i - 1
-            phase0(s).wait()
-            for j in range(2):
-                @pl.loop(0, quarter // 4)
-                def _(g):
-                    ts = pl.ds(quarter * j + g * 4, 4)
-                    sum0[lax.rem(s, 2), ts] = part[pl.ds(base + quarter * j + g * 4, 4)] + recv0[lax.rem(s, 2), ts]
-
-                phase1(s, j).start()
 
         @pl.when(live)
         def _():

time: 180 us -> 183 us (1.017)
  Pallas kernels: 180 us -> 182 us
    pallas_call x1, Pallas kernels: 159 us -> 162 us  [decode_shard(): pl.pallas_call(functools.partial(decode_kernel, n_chunks, n_stages), out_...]
where the time goes in v13:
time: 183 us
  Pallas kernels  182 us (99%)
    pallas_call x1, Pallas kernels, decode_shard(): pl.pallas_call(functools.partial(decode_kernel, n_chunks, n_stages), out_...  162 us
    pallas_call x1, Pallas kernels, decode_shard(): pl.pallas_call(functools.partial(merge_kernel, n_blocks), out_shape=(jax....  20.4 us

profile of v13, /device:TPU:0, one launch (start us, length us, event | category | flops | bytes accessed | tf_op | source)
XLA Modules:
  0.0 182.9 jit_solution(17154996682137418968)
XLA Ops:
  0.6 161.8 %decode.1 = (bf16[32,64,2048]{2,1,0:T(8,128)(2,1)}, bf16[2,64,64,128]{3,2,1,0:T(8,128)(2,1)}, bf16[2,64,64,128]{3,2,1,0:T(8,128)(2,1)}) custom-call(bf16[32,64,2048]{2,1,0:T(8,128)(2,1)} %x_hbm.1, bf16[2,64,256,128]{3,2,1,0:T(8,128)(2,1)} %bitcast.8, bf16[2,64,256,128]{3,2,1,0:T(8,128)(2,1)} %bitcast.10, bf16[2,2048,256]{2,1,0:T(8,128)(2,1)} %wq_hbm.1, ...), custom_call_target="tpu_custom_call" | custom-call | tf_op jit(solution)/shard_map/decode/pallas_call | solution.py:385
  162.5 20.4 %merge.1 = (bf16[32,64,2048]{2,1,0:T(8,128)(2,1)}, bf16[128,128,2,128]{3,2,1,0:T(2,128)(2,1)}, bf16[128,128,2,128]{3,2,1,0:T(2,128)(2,1)}) custom-call(s32[64]{0:T(128)} %lens.1, bf16[32,64,2048]{2,1,0:T(8,128)(2,1)} %get-tuple-element.9.hid_in, bf16[128,128,2,128]{3,2,1,0:T(2,128)(2,1)} %bitcast.9, bf16[128,128,2,128]{3,2,1,0:T(2,128)(2,1)} %bitcast.11, ...), custom_call_target="tpu_custom_call" | custom-call | tf_op jit(solution)/shard_map/merge/pallas_call | solution.py:418

commit v14 on v10

--- a/solution.py
+++ b/solution.py
@@ -339,12 +339,18 @@
         pairs = ((kbuf, k_out), (vbuf, v_out), (hbuf, hid_out))
         return [pltpu.make_async_copy(block(src, i), block(dst, i), out_sem.at[j, i]) for j, (src, dst) in enumerate(pairs)]
 
-    for i in range(n_blocks):
+    ahead = 4
+    for i in range(ahead):
         for copy in loads(i):
             copy.start()
 
     @pl.loop(0, n_blocks)
     def _(i):
+        @pl.when(i + ahead < n_blocks)
+        def _():
+            for copy in loads(i + ahead):
+                copy.start()
+
         for copy in loads(i):
             copy.wait()
         for b in range(size):

time: 180 us -> 180 us (level)
  no operation moved by 1% of the time
where the time goes in v14:
time: 180 us
  Pallas kernels  180 us (100%)
    pallas_call x1, Pallas kernels, decode_shard(): pl.pallas_call(functools.partial(decode_kernel, n_chunks, n_stages), out_...  159 us
    pallas_call x1, Pallas kernels, decode_shard(): pl.pallas_call(functools.partial(merge_kernel, n_blocks), out_shape=(jax....  20.5 us

profile of v14, /device:TPU:0, one launch (start us, length us, event | category | flops | bytes accessed | tf_op | source)
XLA Modules:
  0.0 180.2 jit_solution(2760625081296371492)
XLA Ops:
  0.6 159.1 %decode.1 = (bf16[32,64,2048]{2,1,0:T(8,128)(2,1)}, bf16[2,64,64,128]{3,2,1,0:T(8,128)(2,1)}, bf16[2,64,64,128]{3,2,1,0:T(8,128)(2,1)}) custom-call(bf16[32,64,2048]{2,1,0:T(8,128)(2,1)} %x_hbm.1, bf16[2,64,256,128]{3,2,1,0:T(8,128)(2,1)} %bitcast.8, bf16[2,64,256,128]{3,2,1,0:T(8,128)(2,1)} %bitcast.10, bf16[2,2048,256]{2,1,0:T(8,128)(2,1)} %wq_hbm.1, ...), custom_call_target="tpu_custom_call" | custom-call | tf_op jit(solution)/shard_map/decode/pallas_call | solution.py:389
  159.8 20.5 %merge.1 = (bf16[32,64,2048]{2,1,0:T(8,128)(2,1)}, bf16[128,128,2,128]{3,2,1,0:T(2,128)(2,1)}, bf16[128,128,2,128]{3,2,1,0:T(2,128)(2,1)}) custom-call(s32[64]{0:T(128)} %lens.1, bf16[32,64,2048]{2,1,0:T(8,128)(2,1)} %get-tuple-element.9.hid_in, bf16[128,128,2,128]{3,2,1,0:T(2,128)(2,1)} %bitcast.9, bf16[128,128,2,128]{3,2,1,0:T(2,128)(2,1)} %bitcast.11, ...), custom_call_target="tpu_custom_call" | custom-call | tf_op jit(solution)/shard_map/merge/pallas_call | solution.py:422
